TPU v7x, 32 devices: a whole 2x2x4 slice. The times are simulated.
32 devices in a mesh: seq: 8 (over z, y), batch: 4 (over x, core).
Axes of the slice: x: 2, y: 2, z: 4, core: 2. Of those that a mesh axis runs over, the one named last changes fastest.
Arguments:
- queries: bfloat16 [4, 4096, 16, 128], P('batch', 'seq'), may hold values from -5 to 5
- keys: bfloat16 [4, 4096, 16, 128], P('batch', 'seq'), may hold values from -5 to 5
- values: bfloat16 [4, 4096, 16, 128], P('batch', 'seq'), may hold values from -5 to 5
- keep_count: int32 [4, 16, 32], P('batch'), may hold values from 0 to 128
- query_map: bfloat16 [16, 128, 8], replicated, may hold values from -0.5 to 0.5
- key_map: bfloat16 [16, 128, 8], replicated, may hold values from -0.5 to 0.5
- cotangent: bfloat16 [4, 4096, 16, 128], P('batch', 'seq'), may hold values from -5 to 5
Outputs:
- attended: bfloat16 [4, 4096, 16, 128], P('batch', 'seq')
- grad_query_map: float32 [16, 128, 8], replicated
- grad_key_map: float32 [16, 128, 8], replicated
All inputs are finite; a program needn't handle non-finite values.
Results may differ from a plain program's by a relative error of at most 0.0035.
Values may be sent and summed in bfloat16 or wider, within the bound.
A program may use at most 128 MiB of HBM per device.

v0:
```python
import functools
import math

import jax
import jax.numpy as jnp
from jax import lax
from jax.experimental import pallas as pl
from jax.experimental.pallas import tpu as pltpu
from jax.sharding import PartitionSpec as P

TILE = 128
SHIFT = 1.5
LOG2E = 1.0 / math.log(2.0)
MASKED = -1e30
F32 = jnp.float32
BF16 = jnp.bfloat16
GROUP = 8
VMEM_LIMIT = 56 * 1024 * 1024


def dot_nt(a, b):
    return lax.dot_general(a, b, (((1,), (1,)), ((), ())), preferred_element_type=F32)


def dot_nn(a, b):
    return lax.dot_general(a, b, (((1,), (0,)), ((), ())), preferred_element_type=F32)


def dot_tn(a, b):
    return lax.dot_general(a, b, (((0,), (0,)), ((), ())), preferred_element_type=F32)


def by_head(x):
    return jnp.swapaxes(x, 0, 1)


def softplus(x):
    return jnp.maximum(x, 0.0) + jnp.log1p(jnp.exp(-jnp.abs(x)))


def sigmoid(x):
    return 1.0 / (1.0 + jnp.exp(-x))


def halves(x):
    top = x.astype(BF16)
    return top, (x - top.astype(F32)).astype(BF16)


def split_dot(dot, x, y):
    rows = x.shape[0]
    both = dot(jnp.concatenate(halves(x), 0), y)
    return both[:rows] + both[rows:]


def with_ones(v):
    return jnp.concatenate([v, jnp.ones(v.shape, v.dtype)], 1)


def state_kernel(k_ref, v_ref, wk_ref, kh_ref, vh_ref, total_ref, acc_ref):
    step = pl.program_id(0)
    heads = wk_ref.shape[0]
    kh_ref[...] = by_head(k_ref[...])
    vh_ref[...] = by_head(v_ref[...])

    @pl.when(step == 0)
    def _():
        acc_ref[...] = jnp.zeros_like(acc_ref)

    pre = jnp.stack([dot_nt(wk_ref[h], kh_ref[h]) for h in range(heads)], 0)
    feat = softplus(pre - SHIFT)
    for h in range(heads):
        acc_ref[h] += split_dot(dot_nn, feat[h], with_ones(vh_ref[h]))

    @pl.when(step == pl.num_programs(0) - 1)
    def _():
        total_ref[...] = acc_ref[...]


def local_states(k_rows, v_rows, wk):
    tokens, heads, width = k_rows.shape
    rank = wk.shape[1]
    row_spec = pl.BlockSpec((TILE, heads, width), lambda n: (n, 0, 0))
    head_spec = pl.BlockSpec((heads, TILE, width), lambda n: (0, n, 0))
    return pl.pallas_call(
        state_kernel,
        name="local_states",
        grid=(tokens // TILE,),
        in_specs=[row_spec, row_spec, pl.BlockSpec(wk.shape, lambda n: (0, 0, 0))],
        out_specs=[head_spec, head_spec, pl.BlockSpec((heads, rank, 2 * width), lambda n: (0, 0, 0))],
        out_shape=[
            jax.ShapeDtypeStruct((heads, tokens, width), BF16),
            jax.ShapeDtypeStruct((heads, tokens, width), BF16),
            jax.ShapeDtypeStruct((heads, rank, 2 * width), F32),
        ],
        scratch_shapes=[pltpu.VMEM((heads, rank, 2 * width), F32)],
        compiler_params=pltpu.CompilerParams(vmem_limit_bytes=VMEM_LIMIT),
        cost_estimate=pl.CostEstimate(flops=10**9, bytes_accessed=8 * 2**20, transcendentals=10**6),
    )(k_rows, v_rows, wk)


def main_kernel(
    first, halo, counts_ref, where_ref, q_ref, k_ref, v_ref, kp_ref, vp_ref, c_ref, wq_ref, wk_ref,
    states_ref, *refs,
):
    out_ref, ds_ref, gq_ref, gk_ref, qh, ch, oh, kph, vph, run = refs[-10:]
    step = pl.program_id(0)
    heads = wq_ref.shape[0]
    width = q_ref.shape[2]
    me = where_ref[0]
    tiles_dev = where_ref[1]
    factor = LOG2E / math.sqrt(width)
    qh[...] = by_head(q_ref[...])
    ch[...] = by_head(c_ref[...])
    if halo:
        kph[...] = by_head(kp_ref[...])
        vph[...] = by_head(vp_ref[...])
    prev_k = kph if halo else kp_ref
    prev_v = vph if halo else vp_ref

    @pl.when(step == 0)
    def _():
        gq_ref[...] = jnp.zeros_like(gq_ref)
        gk_ref[...] = jnp.zeros_like(gk_ref)
        run[...] = states_ref[...]

    tile = me * tiles_dev + first + step
    lane = lax.broadcasted_iota(jnp.int32, (1, TILE), 1)
    row = lax.broadcasted_iota(jnp.int32, (TILE, TILE), 0)
    col = lax.broadcasted_iota(jnp.int32, (TILE, TILE), 1)
    causal = col <= row

    def some_heads(g, carry):
        hs = [g * GROUP + i for i in range(GROUP)]
        each = range(GROUP)
        qs, ks, vs = [qh[h] for h in hs], [k_ref[h] for h in hs], [v_ref[h] for h in hs]
        kps, vps = [prev_k[h] for h in hs], [prev_v[h] for h in hs]
        own_raw = [dot_nt(qs[i], ks[i]) for i in each]
        old_raw = [dot_nt(qs[i], kps[i]) for i in each]
        pre_p = [dot_nt(wk_ref[hs[i]], kps[i]) - SHIFT for i in each]
        pre_q = [dot_nt(wq_ref[hs[i]], qs[i]) - SHIFT for i in each]
        counts = [jnp.where(tile > 0, counts_ref[h, jnp.maximum(tile - 1, 0)], 0) for h in hs]
        kept = [lane < count for count in counts]
        kept_f = [keep.astype(F32) for keep in kept]
        own = [jnp.where(causal, own_raw[i], MASKED) for i in each]
        old = [jnp.where(kept[i], old_raw[i], MASKED) for i in each]
        top = [jnp.max(jnp.maximum(own[i], old[i]), 1, keepdims=True) * factor for i in each]
        feat_p = [softplus(pre) for pre in pre_p]
        feat_q = [softplus(pre) for pre in pre_q]
        both = [
            split_dot(dot_nn, jnp.concatenate([feat_p[i], feat_p[i] * kept_f[i]], 0), with_ones(vps[i])) for i in each
        ]
        state = []
        for i in each:
            rank = feat_p[i].shape[0]
            total = run[hs[i]]
            if not halo:
                total += both[i][:rank]
                run[hs[i]] = total
            state.append(total - both[i][rank:])
        p_own = [jnp.exp2(own[i] * factor - top[i]).astype(BF16) for i in each]
        p_old = [jnp.exp2(old[i] * factor - top[i]).astype(BF16) for i in each]
        numer = [dot_nn(p_own[i], with_ones(vs[i])) + dot_nn(p_old[i], with_ones(vps[i])) for i in each]
        decay = [jnp.exp2(-t) for t in top]
        kernel = []
        for i in each:
            fq_top, fq_low = halves(feat_q[i])
            st_top, st_low = halves(state[i])
            kernel.append(
                dot_tn(jnp.concatenate([fq_top, fq_low, fq_top], 0), jnp.concatenate([st_top, st_top, st_low], 0))
            )
        g_ext = []
        for i in each:
            full = numer[i] + decay[i] * kernel[i]
            inv = 1.0 / full[:, width:]
            out = full[:, :width] * inv
            oh[hs[i]] = out.astype(BF16)
            gn = decay[i] * (ch[hs[i]].astype(F32) * inv)
            g_ext.append(jnp.concatenate([gn, gn * out], 1).astype(BF16))
        signed = [jnp.concatenate([st[:, :width], -st[:, width:]], 1) for st in state]
        d_fq = [split_dot(dot_nt, signed[i], g_ext[i]) for i in each]
        ds = [split_dot(dot_nn, feat_q[i], g_ext[i]) for i in each]
        dpre_q = [d_fq[i] * sigmoid(pre_q[i]) for i in each]
        d_fk = [
            split_dot(dot_nt, ds[i][:, :width], vps[i]) - jnp.sum(ds[i][:, width:], 1, keepdims=True) for i in each
        ]
        dpre_k = [-kept_f[i] * d_fk[i] * sigmoid(pre_p[i]) for i in each]
        gq = [split_dot(dot_nn, dpre_q[i], qs[i]) for i in each]
        gk = [split_dot(dot_nn, dpre_k[i], kps[i]) for i in each]
        for i in each:
            ds_ref[0, hs[i]] = ds[i]
            gq_ref[hs[i]] += gq[i]
            gk_ref[hs[i]] += gk[i]
        return carry

    lax.fori_loop(0, heads // GROUP, some_heads, 0)
    out_ref[...] = by_head(oh[...])


def attend(first, steps, begun, counts, where, q_rows, kh, vh, kp, vp, cot, wq, wk, states):
    tokens, heads, width = q_rows.shape
    rank = wq.shape[1]
    row_spec = pl.BlockSpec((TILE, heads, width), lambda n: (n + first, 0, 0))
    head_spec = pl.BlockSpec((heads, TILE, width), lambda n: (0, n + first, 0))
    halo = begun is not None
    if halo:
        prev_specs = [pl.BlockSpec((None, TILE, heads, width), lambda n, i=i: (i, 0, 0, 0)) for i in range(2)]
    else:
        prev_specs = [pl.BlockSpec((heads, TILE, width), lambda n: (0, n + first - 1, 0))] * 2
    whole = pl.BlockSpec((heads, rank, width), lambda n: (0, 0, 0))
    smem = pl.BlockSpec(memory_space=pltpu.SMEM)
    tile_scratch = pltpu.VMEM((heads, TILE, width), BF16)
    return pl.pallas_call(
        functools.partial(main_kernel, first, halo),
        name="attend_first" if halo else "attend_rest",
        grid=(steps,),
        in_specs=[
            smem, smem, row_spec, head_spec, head_spec, *prev_specs, row_spec, whole, whole,
            pl.BlockSpec(states.shape, lambda n: (0, 0, 0)),
        ] + [pl.BlockSpec(memory_space=pl.ANY)] * halo,
        out_specs=[
            row_spec,
            pl.BlockSpec((1, heads, rank, 2 * width), lambda n: (n, 0, 0, 0)),
            whole,
            whole,
        ],
        out_shape=[
            jax.ShapeDtypeStruct((tokens, heads, width), BF16),
            jax.ShapeDtypeStruct((steps, heads, rank, 2 * width), F32),
            jax.ShapeDtypeStruct((heads, rank, width), F32),
            jax.ShapeDtypeStruct((heads, rank, width), F32),
        ],
        scratch_shapes=[tile_scratch] * 5 + [pltpu.VMEM((heads, rank, 2 * width), F32)],
        compiler_params=pltpu.CompilerParams(vmem_limit_bytes=VMEM_LIMIT),
        cost_estimate=pl.CostEstimate(flops=10**9 * steps, bytes_accessed=steps * 4 * 2**20, transcendentals=10**6),
        input_output_aliases={11: 0} if halo else {},
    )(counts, where, q_rows, kh, vh, kp, vp, cot, wq, wk, states, *([begun] if halo else []))


def key_kernel(kh_ref, vh_ref, wk_ref, ds1_ref, after_ref, gk_ref):
    group, tokens, width = kh_ref.shape
    tiles = tokens // TILE
    each = range(group)
    pre = [dot_nt(wk_ref[h], kh_ref[h]) - SHIFT for h in each]
    grads = []
    for h in each:
        later = after_ref[h][:, :width]
        norm = after_ref[h][:, width:]
        pieces = [None] * tiles
        for n in reversed(range(tiles)):
            pieces[n] = split_dot(dot_nt, later, vh_ref[h, n * TILE : (n + 1) * TILE]) + norm
            if n:
                later += ds1_ref[n - 1, h][:, :width]
                norm -= jnp.sum(ds1_ref[n - 1, h][:, width:], 1, keepdims=True)
        grads.append(jnp.concatenate(pieces, 1))
    for h in each:
        gk_ref[h] = split_dot(dot_nn, grads[h] * sigmoid(pre[h]), kh_ref[h])


def flat_id(axes):
    index, count = 0, 1
    for axis in axes:
        index = index * lax.axis_size(axis) + lax.axis_index(axis)
        count *= lax.axis_size(axis)
    return index, count


def place(flat, axes):
    where = {}
    for axis in reversed(axes):
        size = lax.axis_size(axis)
        where[axis] = lax.rem(flat, size)
        flat = flat // size
    return where


def greet(count, me, axes):
    barrier = pltpu.get_barrier_semaphore()

    def hello(i, carry):
        pl.semaphore_signal(
            barrier, inc=1, device_id=place(lax.rem(me + i, count), axes), device_id_type=pl.DeviceIdType.MESH
        )
        return carry

    lax.fori_loop(1, count, hello, 0)
    return barrier


def others_kernel(axis, later, *refs):
    parts, (out_ref, mine, slots, send_sem, recv_sem) = refs[:-5], refs[-5:]
    heads, _, twice = out_ref.shape
    width = twice // 2
    axes = (axis,)
    me, count = flat_id(axes)
    barrier = greet(count, me, axes)
    lane = lax.broadcasted_iota(jnp.int32, (1, width), 1)
    packed = jnp.zeros(mine.shape[1:], F32)
    shape = mine.shape
    for h in range(heads):
        own = sum(part[n, h] for part in parts for n in range(part.shape[0]))
        mine[h] = own[:, :width].astype(BF16)
        norm = -jnp.sum(own[:, width:], 1, keepdims=True) if later else own[:, width:]
        packed = jnp.where(lane == h, norm, packed)
    mine[heads], mine[heads + 1] = halves(packed)
    pl.semaphore_wait(barrier, count - 1)

    def copy(sender, target):
        return pltpu.make_async_remote_copy(
            src_ref=mine,
            dst_ref=slots.at[sender],
            send_sem=send_sem.at[target],
            recv_sem=recv_sem.at[sender],
            device_id=place(target, axes),
            device_id_type=pl.DeviceIdType.MESH,
        )

    if later:
        first_to, end_to, first_from, end_from = 0, me, me + 1, count
    else:
        first_to, end_to, first_from, end_from = me + 1, count, 0, me

    def send(p, carry):
        copy(me, p).start()
        return carry

    def sent(p, carry):
        copy(me, p).wait_send()
        return carry

    def received(p, total):
        copy(p, lax.rem(me + 1, count)).wait_recv()
        return total + slots[p].astype(F32)

    lax.fori_loop(first_to, end_to, send, 0)
    total = lax.fori_loop(first_from, end_from, received, jnp.zeros(shape, F32))
    lax.fori_loop(first_to, end_to, sent, 0)
    for h in range(heads):
        norm = jnp.sum(jnp.where(lane == h, total[heads] + total[heads + 1], 0.0), 1, keepdims=True)
        out_ref[h] = jnp.concatenate([total[h], jnp.broadcast_to(norm, total[h].shape)], 1)


def sum_of_others(parts, axis, later, collective_id):
    heads, rank, twice = parts[0].shape[1:]
    count = lax.axis_size(axis)
    block = (heads + 2, rank, twice // 2)
    vmem = pl.BlockSpec(memory_space=pltpu.VMEM)
    return pl.pallas_call(
        functools.partial(others_kernel, axis, later),
        name="later_grads" if later else "earlier_states",
        in_specs=[vmem] * len(parts),
        out_specs=vmem,
        out_shape=jax.ShapeDtypeStruct((heads, rank, twice), F32),
        scratch_shapes=[
            pltpu.VMEM(block, BF16),
            pltpu.VMEM((count,) + block, BF16),
            pltpu.SemaphoreType.DMA((count,)),
            pltpu.SemaphoreType.DMA((count,)),
        ],
        compiler_params=pltpu.CompilerParams(
            collective_id=collective_id, has_side_effects=True, vmem_limit_bytes=VMEM_LIMIT
        ),
        cost_estimate=pl.CostEstimate(flops=10**7, bytes_accessed=2**20, transcendentals=0),
    )(*parts)


def reduce_kernel(axes, gq0, gq1, gk0, gk1, gk2, gq_ref, gk_ref, mine, slots, done, out_sem, in_sem, back_sem, res_sem):
    heads = gq0.shape[0]
    chunks = 2 * heads
    me, count = flat_id(axes)
    owners = min(count, chunks)
    stride, per = count // owners, chunks // owners
    barrier = greet(count, me, axes)
    mine[:heads] = gq0[...] + gq1[...]
    mine[heads:] = gk0[...] + gk1[...] + gk2[...]
    pl.semaphore_wait(barrier, count - 1)
    owner = lax.rem(me, stride) == 0
    part = me // stride

    def to_owner(o, sender):
        return pltpu.make_async_remote_copy(
            src_ref=mine.at[pl.ds(o * per, per)],
            dst_ref=slots.at[sender],
            send_sem=out_sem.at[o],
            recv_sem=in_sem.at[sender],
            device_id=place(o * stride, axes),
            device_id_type=pl.DeviceIdType.MESH,
        )

    def to_all(o, target):
        return pltpu.make_async_remote_copy(
            src_ref=done.at[pl.ds(o * per, per)],
            dst_ref=done.at[pl.ds(o * per, per)],
            send_sem=back_sem.at[target],
            recv_sem=res_sem.at[o],
            device_id=place(target, axes),
            device_id_type=pl.DeviceIdType.MESH,
        )

    def over_owners(act):
        def step(i, carry):
            o = lax.rem(part + i, owners)

            @pl.when(o * stride != me)
            def _():
                act(o)

            return carry

        lax.fori_loop(0, owners, step, 0)

    over_owners(lambda o: to_owner(o, me).start())

    @pl.when(owner)
    def _():
        def arrived(i, total):
            sender = lax.rem(me + i, count)
            to_owner(part, sender).wait_recv()
            return total + slots[sender]

        done[pl.ds(part * per, per)] = lax.fori_loop(1, count, arrived, mine[pl.ds(part * per, per)])

        def send(i, carry):
            to_all(part, lax.rem(me + i, count)).start()
            return carry

        lax.fori_loop(1, count, send, 0)

    over_owners(lambda o: to_owner(o, me).wait_send())
    over_owners(lambda o: to_all(o, lax.rem(me + 1, count)).wait_recv())

    @pl.when(owner)
    def _():
        def sent(i, carry):
            to_all(part, lax.rem(me + i, count)).wait_send()
            return carry

        lax.fori_loop(1, count, sent, 0)

    gq_ref[...] = done[:heads]
    gk_ref[...] = done[heads:]


def sum_over_all(grads, axes):
    heads, rank, width = grads[0].shape
    count = math.prod(lax.axis_size(axis) for axis in axes)
    owners = min(count, 2 * heads)
    per = 2 * heads // owners
    vmem = pl.BlockSpec(memory_space=pltpu.VMEM)
    whole = (2 * heads, rank, width)
    return pl.pallas_call(
        functools.partial(reduce_kernel, axes),
        name="sum_grads",
        in_specs=[vmem] * len(grads),
        out_specs=[vmem, vmem],
        out_shape=[jax.ShapeDtypeStruct((heads, rank, width), F32)] * 2,
        scratch_shapes=[
            pltpu.VMEM(whole, F32),
            pltpu.VMEM((count, per, rank, width), F32),
            pltpu.VMEM(whole, F32),
            pltpu.SemaphoreType.DMA((owners,)),
            pltpu.SemaphoreType.DMA((count,)),
            pltpu.SemaphoreType.DMA((count,)),
            pltpu.SemaphoreType.DMA((owners,)),
        ],
        compiler_params=pltpu.CompilerParams(collective_id=2, has_side_effects=True, vmem_limit_bytes=VMEM_LIMIT),
        cost_estimate=pl.CostEstimate(flops=10**7, bytes_accessed=2**20, transcendentals=0),
    )(*grads)


def key_grads(kh, vh, wk, ds1, after):
    heads, tokens, width = kh.shape
    rank = wk.shape[1]
    group = 4
    head_spec = pl.BlockSpec((group, tokens, width), lambda n: (n, 0, 0))
    whole = pl.BlockSpec((group, rank, width), lambda n: (n, 0, 0))
    four = pl.BlockSpec((ds1.shape[0], group, rank, 2 * width), lambda n: (0, n, 0, 0))

    return pl.pallas_call(
        key_kernel,
        name="key_grads",
        grid=(heads // group,),
        in_specs=[
            head_spec, head_spec, whole, four, pl.BlockSpec((group, rank, 2 * width), lambda n: (n, 0, 0)),
        ],
        out_specs=whole,
        out_shape=jax.ShapeDtypeStruct((heads, rank, width), F32),
        compiler_params=pltpu.CompilerParams(vmem_limit_bytes=VMEM_LIMIT),
        cost_estimate=pl.CostEstimate(flops=10**9, bytes_accessed=8 * 2**20, transcendentals=10**6),
    )(kh, vh, wk, ds1, after)


def body(queries, keys, values, keep_count, query_map, key_map, cotangent):
    q_rows, k_rows, v_rows, cot = queries[0], keys[0], values[0], cotangent[0]
    counts = keep_count[0]
    tokens = q_rows.shape[0]
    tiles = tokens // TILE
    peers = lax.axis_size("seq")
    me = lax.axis_index("seq")
    where = jnp.stack([me, jnp.int32(tiles)]).astype(jnp.int32)
    ring = [(a, a + 1) for a in range(peers - 1)]
    halo = lax.ppermute(jnp.stack([k_rows[tokens - TILE :], v_rows[tokens - TILE :]]), "seq", ring)
    wq = jnp.swapaxes(query_map, 1, 2)
    wk = jnp.swapaxes(key_map, 1, 2)
    kh, vh, total = local_states(k_rows, v_rows, wk)
    states = sum_of_others([total[None]], "seq", False, 0)
    rest = attend(1, tiles - 1, None, counts, where, q_rows, kh, vh, kh, vh, cot, wq, wk, states)
    head = attend(0, 1, rest[0], counts, where, q_rows, kh, vh, halo, halo, cot, wq, wk, states)
    after = sum_of_others([head[1], rest[1]], "seq", True, 1)
    gk = key_grads(kh, vh, wk, rest[1], after)
    grads = sum_over_all([head[2], rest[2], head[3], rest[3], gk], ("seq", "batch"))
    return head[0][None], jnp.swapaxes(grads[0], 1, 2), jnp.swapaxes(grads[1], 1, 2)


def solution(mesh):
    placed = (
        P("batch", "seq", None, None),
        P("batch", "seq", None, None),
        P("batch", "seq", None, None),
        P("batch", None, None),
        P(),
        P(),
        P("batch", "seq", None, None),
    )
    return jax.shard_map(
        body,
        mesh=mesh,
        in_specs=placed,
        out_specs=(P("batch", "seq", None, None), P(), P()),
        check_vma=False,
    )
```

profile of v0, /device:TPU:0, one launch (start us, length us, event | category | flops | bytes accessed | tf_op | source)
XLA Modules:
  0.0 98.1 jit_solution(555866390427515050)
XLA Ops:
  0.6 0.0 slice-start
  0.6 0.0 slice-start.1
  0.7 1.0 %slice-done = bf16[1,128,16,128]{3,2,1,0:T(8,128)(2,1)S(1)} async-done(((bf16[1,512,16,128]{3,2,1,0:T(8,128)(2,1)}), bf16[1,128,16,128]{3,2,1,0:T(8,128)(2,1)S(1)}, s32[]{:S(2)}) %slice-start) | async-done | bytes 524312 | tf_op jit(solution)/shard_map/slice | solution.py:502
  1.7 0.2 slice-done.1
  1.8 0.1 pad_maximum_fusion
  1.9 5.0 %collective-permute-start = (bf16[2,128,16,128]{3,2,1,0:T(8,128)(2,1)S(1)}, bf16[2,128,16,128]{3,2,1,0:T(8,128)(2,1)S(1)}, u32[]{:S(2)}, u32[]{:S(2)}) collective-permute-start(bf16[2,128,16,128]{3,2,1,0:T(8,128)(2,1)S(1)} %pad_maximum_fusion), channel_id=1, source_target_pairs={{0,4},{4,8},{8,12},{12,16},{16,20},{20,24},{24,28},{1,5},{5,9},{9,... | collective-permute-start | bytes 3145736 | tf_op jit(solution)/shard_map/ppermute | solution.py:502
  6.9 6.3 %local_states.1 = (bf16[16,512,128]{2,1,0:T(8,128)(2,1)}, bf16[16,512,128]{2,1,0:T(8,128)(2,1)}, f32[16,8,256]{2,1,0:T(8,128)}) custom-call(bf16[512,16,128]{2,1,0:T(8,128)(2,1)} %bitcast.16, bf16[512,16,128]{2,1,0:T(8,128)(2,1)} %bitcast.17, bf16[16,8,128]{2,1,0:T(8,128)(2,1)} %bitcast.19), custom_call_target="tpu_custom_call" | custom-call | flops 1000000000 | bytes 8388608 | tf_op jit(solution)/shard_map/local_states/pallas_call | solution.py:85
  13.2 17.7 %earlier_states.1.states_ref = f32[16,8,256]{2,1,0:T(8,128)} custom-call(f32[1,16,8,256]{3,2,1,0:T(8,128)} %bitcast.25), custom_call_target="tpu_custom_call" | custom-call | flops 10000000 | bytes 1048576 | tf_op jit(solution)/shard_map/earlier_states/pallas_call | solution.py:348
  30.9 0.6 pad_add_fusion.where_ref
  31.5 15.2 %attend_rest.1 = (bf16[512,16,128]{2,1,0:T(8,128)(2,1)}, f32[3,16,8,256]{3,2,1,0:T(8,128)}, f32[16,8,128]{2,1,0:T(8,128)}, f32[16,8,128]{2,1,0:T(8,128)}) custom-call(s32[16,32]{1,0:T(8,128)} %bitcast.28, s32[2]{0:T(128)} %pad_add_fusion.where_ref, bf16[512,16,128]{2,1,0:T(8,128)(2,1)} %bitcast.12, ...), custom_call_target="tpu_custom_call" | custom-call | flops 3000000000 | bytes 12582912 | tf_op jit(solution)/shard_map/attend_rest/pallas_call | solution.py:213
  46.7 0.0 collective-permute-done.kp_ref.vp_ref
  46.8 0.0 copy-start
  46.8 1.0 copy-done
  47.7 7.1 %attend_first.1 = (bf16[512,16,128]{2,1,0:T(8,128)(2,1)}, f32[1,16,8,256]{3,2,1,0:T(8,128)}, f32[16,8,128]{2,1,0:T(8,128)}, f32[16,8,128]{2,1,0:T(8,128)}) custom-call(s32[16,32]{1,0:T(8,128)} %bitcast.29, s32[2]{0:T(128)} %pad_add_fusion.where_ref, bf16[512,16,128]{2,1,0:T(8,128)(2,1)} %bitcast.13, ...), custom_call_target="tpu_custom_call", output_to_operand_aliasing={{0}: (11, {})} | custom-call | flops 1000000000 | bytes 4194304 | tf_op jit(solution)/shard_map/attend_first/pallas_call | solution.py:213
  54.9 17.7 %later_grads.1.after_ref = f32[16,8,256]{2,1,0:T(8,128)} custom-call(f32[1,16,8,256]{3,2,1,0:T(8,128)} %get-tuple-element.26.refs_0_, f32[3,16,8,256]{3,2,1,0:T(8,128)} %get-tuple-element.25.refs_1_.ds1_ref), custom_call_target="tpu_custom_call" | custom-call | flops 10000000 | bytes 1048576 | tf_op jit(solution)/shard_map/later_grads/pallas_call | solution.py:348
  72.5 5.1 %key_grads.1.gk2 = f32[16,8,128]{2,1,0:T(8,128)} custom-call(bf16[16,512,128]{2,1,0:T(8,128)(2,1)} %get-tuple-element.16.k_ref.kp_ref.kh_ref, bf16[16,512,128]{2,1,0:T(8,128)(2,1)} %get-tuple-element.17.v_ref.vp_ref.vh_ref, bf16[16,8,128]{2,1,0:T(8,128)(2,1)} %bitcast.22, f32[3,16,8,256]{3,2,1,0:T(8,128)} %get-tuple-element.25.refs_1_.ds1_ref, ...), custom_call_target="tpu_custom_call" | custom-call | flops 1000000000 | bytes 8388608 | tf_op jit(solution)/shard_map/key_grads/pallas_call | solution.py:479
  77.6 17.5 %sum_grads.1 = (f32[16,8,128]{2,1,0:T(8,128)}, f32[16,8,128]{2,1,0:T(8,128)}) custom-call(f32[16,8,128]{2,1,0:T(8,128)} %get-tuple-element.21.gq0, f32[16,8,128]{2,1,0:T(8,128)} %get-tuple-element.22.gq1, f32[16,8,128]{2,1,0:T(8,128)} %get-tuple-element.23.gk0, f32[16,8,128]{2,1,0:T(8,128)} %get-tuple-element.24.gk1, f32[16,8,128]{2,1,0:T(8,128)} %key_grads.1.gk2), custom_call_target="tpu_custom_call" | custom-call | flops 10000000 | bytes 1048576 | tf_op jit(solution)/shard_map/sum_grads/pallas_call | solution.py:451
  95.2 1.5 %copy.14 = f32[16,128,8]{1,2,0:T(8,128)} copy(f32[16,128,8]{1,2,0:T(8,128)} %bitcast.27) | data formatting | bytes 131072
  96.6 1.5 %copy.15 = f32[16,128,8]{1,2,0:T(8,128)} copy(f32[16,128,8]{1,2,0:T(8,128)} %bitcast.26) | data formatting | bytes 131072
Async XLA Ops:
  0.6 1.0 %slice-start = ((bf16[1,512,16,128]{3,2,1,0:T(8,128)(2,1)}), bf16[1,128,16,128]{3,2,1,0:T(8,128)(2,1)S(1)}, s32[]{:S(2)}) async-start(bf16[1,512,16,128]{3,2,1,0:T(8,128)(2,1)} %param.8), calls=%async_computation | async-start | bytes 1048576 | tf_op jit(solution)/shard_map/slice | solution.py:502
  0.6 1.2 %slice-start.1 = ((bf16[1,512,16,128]{3,2,1,0:T(8,128)(2,1)}), bf16[1,128,16,128]{3,2,1,0:T(8,128)(2,1)S(1)}, s32[]{:S(2)}) async-start(bf16[1,512,16,128]{3,2,1,0:T(8,128)(2,1)} %param.9), calls=%async_computation.1 | async-start | bytes 1048576 | tf_op jit(solution)/shard_map/slice | solution.py:502
  1.9 44.8 %collective-permute-start = (bf16[2,128,16,128]{3,2,1,0:T(8,128)(2,1)S(1)}, bf16[2,128,16,128]{3,2,1,0:T(8,128)(2,1)S(1)}, u32[]{:S(2)}, u32[]{:S(2)}) collective-permute-start(bf16[2,128,16,128]{3,2,1,0:T(8,128)(2,1)S(1)} %pad_maximum_fusion), channel_id=1, source_target_pairs={{0,4},{4,8},{8,12},{12,16},{16,20},{20,24},{24,28},{1,5},{5,9},{9,... | collective-permute-start | bytes 3145736 | tf_op jit(solution)/shard_map/ppermute | solution.py:502
  46.8 1.0 copy-start
where the time goes:
time: 98.6 us; the launch traced here: 98.1 us
  Pallas kernels  86.7 us (88%)
  local copies, waits for them, and re-layouts  5.09 us (5%)
  starting transfers between devices  4.97 us (5%)
    pallas_call x2, Pallas kernels, sum_of_others(): pl.pallas_call(functools.partial(others_kernel, axis, later), name='later...  35.4 us
    pallas_call x2, Pallas kernels, attend(): pl.pallas_call(functools.partial(main_kernel, first, halo), name='attend_...  22.4 us
    pallas_call x1, Pallas kernels, sum_over_all(): pl.pallas_call(functools.partial(reduce_kernel, axes), name='sum_grads',...  17.5 us
    pallas_call x1, Pallas kernels, local_states(): pl.pallas_call(state_kernel, name='local_states', grid=(tokens // TILE,),...  6.32 us
    pallas_call x1, Pallas kernels, key_grads(): pl.pallas_call(key_kernel, name='key_grads', grid=(heads // group,), in_s...  5.12 us
    ppermute x1, starting transfers between devices, body(): lax.ppermute(jnp.stack([k_rows[tokens - TILE:], v_rows[tokens - TILE:]]),...  4.97 us
    unnamed x4, local copies, waits for them, and re-layouts  3.9 us
  transfers between devices with their start and end apart: 1, of which 0 were waited for; matrix products, arithmetic and copies ran while one was open for 1% of the time, Pallas kernels for 40%

commit v1 on v0

v1 whole, which is shorter than its diff:
```python
import functools
import math

import jax
import jax.numpy as jnp
from jax import lax
from jax.experimental import pallas as pl
from jax.experimental.pallas import tpu as pltpu
from jax.sharding import PartitionSpec as P

TILE = 128
SHIFT = 1.5
LOG2E = 1.0 / math.log(2.0)
MASKED = -1e30
F32 = jnp.float32
BF16 = jnp.bfloat16
GROUPS = 2
UNROLL = 4
VMEM_LIMIT = 56 * 1024 * 1024


def dot_nt(a, b):
    return lax.dot_general(a, b, (((1,), (1,)), ((), ())), preferred_element_type=F32)


def dot_nn(a, b):
    return lax.dot_general(a, b, (((1,), (0,)), ((), ())), preferred_element_type=F32)


def dot_tn(a, b):
    return lax.dot_general(a, b, (((0,), (0,)), ((), ())), preferred_element_type=F32)


def by_head(x):
    return jnp.swapaxes(x, 0, 1)


def softplus(x):
    return jnp.maximum(x, 0.0) + jnp.log1p(jnp.exp(-jnp.abs(x)))


def sigmoid(x):
    return 1.0 / (1.0 + jnp.exp(-x))


def halves(x):
    top = x.astype(BF16)
    return top, (x - top.astype(F32)).astype(BF16)


def split_dot(dot, x, y):
    rows = x.shape[0]
    both = dot(jnp.concatenate(halves(x), 0), y)
    return both[:rows] + both[rows:]


def flat_id(axes):
    index, count = 0, 1
    for axis in axes:
        index = index * lax.axis_size(axis) + lax.axis_index(axis)
        count *= lax.axis_size(axis)
    return index, count


def place(flat, axes):
    where = {}
    for axis in reversed(axes):
        size = lax.axis_size(axis)
        where[axis] = lax.rem(flat, size)
        flat = flat // size
    return where


def greet(count, me, axes):
    barrier = pltpu.get_barrier_semaphore()

    def hello(i, carry):
        pl.semaphore_signal(
            barrier, inc=1, device_id=place(lax.rem(me + i, count), axes), device_id_type=pl.DeviceIdType.MESH
        )
        return carry

    lax.fori_loop(1, count, hello, 0)
    return barrier


def at(tile, count=1):
    return pl.ds(tile * TILE, count * TILE)


def owners_of(count, chunks):
    owners = min(count, chunks)
    return owners, count // owners, chunks // owners


def layer_kernel(
    seq, axes, counts_ref, q_hbm, k_hbm, v_hbm, c_hbm, wq_ref, wk_ref, out_hbm, gq_ref, gk_ref,
    qin, kin, vin, cin, kx, vx, vt, qx, ct, oh, halo, num, rows, preq, sigk, sall, nall, skept, nkept,
    sin, nin, dsb, dnb, gaf, naf, mine, slots, grads, gslots, done,
    in_sem, halo_out, halo_in, msg_out, msg_in, red_out, red_in, back_out, back_in, out_sem,
):
    tokens, heads, width = q_hbm.shape
    rank = wq_ref.shape[1]
    tiles = tokens // TILE
    per_group = heads // GROUPS
    factor = LOG2E / math.sqrt(width)
    me = lax.axis_index(seq)
    peers = lax.axis_size(seq)
    flat, count = flat_id(axes)
    sq = (seq,)
    barrier = greet(count, flat, axes)
    base = me * tiles
    lane = lax.broadcasted_iota(jnp.int32, (1, TILE), 1)
    sub = lax.broadcasted_iota(jnp.int32, (TILE, TILE), 0)
    causal = sub <= lax.broadcasted_iota(jnp.int32, (TILE, TILE), 1)

    def load(i, hbm, vmem, n):
        return pltpu.make_async_copy(hbm.at[at(n)], vmem.at[at(n)], in_sem.at[i, n])

    loads = [(k_hbm, kin), (v_hbm, vin), (q_hbm, qin), (c_hbm, cin)]
    for i, (hbm, vmem) in enumerate(loads):
        for n in range(tiles):
            load(i, hbm, vmem, n).start()

    def loaded(i, n):
        load(i, *loads[i], n).wait()

    @pl.when(me == 0)
    def _():
        halo[...] = jnp.zeros_like(halo)

    pl.semaphore_wait(barrier, count - 1)

    def halo_copy(g, i):
        hbm = (k_hbm, v_hbm)[i]
        return pltpu.make_async_remote_copy(
            src_ref=hbm.at[pl.ds(tokens - TILE, TILE), pl.ds(g * per_group, per_group)],
            dst_ref=halo.at[g, i],
            send_sem=halo_out.at[g, i],
            recv_sem=halo_in.at[g, i],
            device_id=place(lax.rem(me + 1, peers), sq),
            device_id_type=pl.DeviceIdType.MESH,
        )

    def halo_start(g):
        @pl.when(me < peers - 1)
        def _():
            halo_copy(g, 0).start()
            halo_copy(g, 1).start()

    def count_before(h, e):
        if e:
            return counts_ref[h, base + e - 1]
        return jnp.where(me > 0, counts_ref[h, jnp.maximum(base - 1, 0)], 0)

    def message(later, g, sender, target):
        return pltpu.make_async_remote_copy(
            src_ref=mine.at[later, g],
            dst_ref=slots.at[later, g, sender],
            send_sem=msg_out.at[later, g, target],
            recv_sem=msg_in.at[later, g, sender],
            device_id=place(target, sq),
            device_id_type=pl.DeviceIdType.MESH,
        )

    def message_start(later, g, state, norm):
        packed = jnp.zeros((rank, width), F32)
        for i in range(per_group):
            mine[later, g, i] = state(g * per_group + i).astype(BF16)
            packed = jnp.where(lane == i, norm(g * per_group + i), packed)
        mine[later, g, per_group], mine[later, g, per_group + 1] = halves(packed)

        def send(p, carry):
            message(later, g, me, p).start()
            return carry

        lax.fori_loop(0 if later else me + 1, me if later else peers, send, 0)

    def message_sent(later, g):
        def sent(p, carry):
            message(later, g, me, p).wait_send()
            return carry

        lax.fori_loop(0 if later else me + 1, me if later else peers, sent, 0)

    def message_sum(later, g, state_ref, norm_ref):
        def received(p, total):
            message(later, g, p, lax.rem(me + 1, peers)).wait_recv()
            return total + slots[later, g, p].astype(F32)

        total = lax.fori_loop(
            me + 1 if later else 0, peers if later else me, received, jnp.zeros((per_group + 2, rank, width), F32)
        )
        norms = total[per_group] + total[per_group + 1]
        for i in range(per_group):
            state_ref[g * per_group + i] = total[i]
            norm = jnp.sum(jnp.where(lane == i, norms, 0.0), 1, keepdims=True)
            norm_ref[g * per_group + i] = jnp.broadcast_to(norm, (rank, width))

    def spread(x):
        return jnp.broadcast_to(jnp.sum(x, 1, keepdims=True), (rank, width))

    def over_heads(first, last, step, act):
        def block(i, carry):
            act([first + i * step + u for u in range(step)])
            return carry

        lax.fori_loop(0, (last - first) // step, block, 0)

    halo_start(0)

    for n in range(tiles):
        loaded(0, n)
        kx[:, at(n + 1)] = by_head(kin[at(n)])
    for n in range(tiles):
        loaded(1, n)
        vx[:, at(n + 1)] = by_head(vin[at(n)])

    def key_states(hs, tile_list):
        first, size = tile_list[0], len(tile_list)
        pre = [dot_nt(wk_ref[h], kx[h, at(first, size)]) - SHIFT for h in hs]
        feat = [softplus(p) for p in pre]
        for h, p in zip(hs, pre):
            sigk[h, :, at(first, size)] = sigmoid(p)
        for e in tile_list:
            cut = slice((e - first) * TILE, (e - first + 1) * TILE)
            own = [f[:, cut] for f in feat]
            if e < tiles:
                kept = [own[i] * (lane < count_before(h, e)).astype(F32) for i, h in enumerate(hs)]
                both = [split_dot(dot_nn, jnp.concatenate([o, k], 0), vx[h, at(e)]) for o, k, h in zip(own, kept, hs)]
                for i, h in enumerate(hs):
                    skept[e, h] = both[i][rank:]
                    nkept[e, h] = spread(kept[i])
            else:
                both = [split_dot(dot_nn, o, vx[h, at(e)]) for o, h in zip(own, hs)]
            if e:
                for i, h in enumerate(hs):
                    sall[e, h] = both[i][:rank]
                    nall[e, h] = spread(own[i])

    ext = list(range(1, tiles + 1))
    for g in range(GROUPS):
        over_heads(g * per_group, (g + 1) * per_group, UNROLL, lambda hs: key_states(hs, ext))
        message_start(
            0, g, lambda h: sum(sall[e, h] for e in ext), lambda h: sum(nall[e, h] for e in ext)
        )
    for g in range(1, GROUPS):
        halo_start(g)

    def flip_values(hs, tile_list):
        for h in hs:
            for e in tile_list:
                vt[h, :, at(e)] = vx[h, at(e)].T

    over_heads(0, heads, UNROLL, lambda hs: flip_values(hs, ext))
    for n in range(tiles):
        loaded(2, n)
        qx[:, at(n)] = by_head(qin[at(n)])

    def query_features(hs):
        pre = [dot_nt(wq_ref[h], qx[h]) - SHIFT for h in hs]
        for h, p in zip(hs, pre):
            preq[h] = p

    over_heads(0, heads, UNROLL, query_features)

    def sparse(hs, j):
        each = range(len(hs))
        scores = [dot_nt(kx[h, at(j - 1, 2)], qx[h, at(j - 1)]) for h in hs]
        old = [jnp.where(sub < count_before(h, j - 1), scores[i][:TILE], MASKED) for i, h in enumerate(hs)]
        own = [jnp.where(causal, scores[i][TILE:], MASKED) for i in each]
        top = [jnp.max(jnp.maximum(old[i], own[i]), 0, keepdims=True) * factor for i in each]
        old = [jnp.exp2(old[i] * factor - top[i]) for i in each]
        own = [jnp.exp2(own[i] * factor - top[i]) for i in each]
        den = [jnp.sum(old[i] + own[i], 0, keepdims=True) for i in each]
        prob = [jnp.concatenate([old[i].astype(BF16), own[i].astype(BF16)], 0) for i in each]
        numer = [dot_nn(vt[h, :, at(j - 1, 2)], prob[i]) for i, h in enumerate(hs)]
        for i, h in enumerate(hs):
            num[h, :, at(j - 1)] = numer[i]
            rows[h, 0:1, at(j - 1)] = den[i]
            rows[h, 1:2, at(j - 1)] = top[i]

    for j in range(2, tiles + 1):
        over_heads(0, heads, UNROLL, lambda hs, j=j: sparse(hs, j))

    for n in range(tiles):
        loaded(3, n)
        oh[:, at(n)] = by_head(cin[at(n)])

    def flip_cotangent(hs):
        for h in hs:
            for n in range(tiles):
                ct[h, :, at(n)] = oh[h, at(n)].T

    over_heads(0, heads, UNROLL, flip_cotangent)
    for g in range(GROUPS):
        message_sum(0, g, sin, nin)

    def combine(hs, j):
        each = range(len(hs))
        where = at(j - 1)
        pre = [preq[h, :, where] for h in hs]
        feat = [softplus(p) for p in pre]
        state = [sum([sall[e, h] for e in range(1, j)], sin[h]) - skept[j - 1, h] for h in hs]
        norm = [sum([nall[e, h] for e in range(1, j)], nin[h]) - nkept[j - 1, h] for h in hs]
        decay = [jnp.exp2(-rows[h, 1:2, where]) for h in hs]
        kernel = []
        for i in each:
            fq_top, fq_low = halves(feat[i])
            st_top, st_low = halves(state[i])
            kernel.append(
                dot_tn(jnp.concatenate([st_top, st_top, st_low], 0), jnp.concatenate([fq_top, fq_low, fq_top], 0))
            )
        den = [jnp.sum(norm[i] * feat[i], 0, keepdims=True) for i in each]
        inv = [1.0 / (rows[h, 0:1, where] + decay[i] * den[i]) for i, h in enumerate(hs)]
        out = [(num[h, :, where] + decay[i] * kernel[i]) * inv[i] for i, h in enumerate(hs)]
        grad = [ct[h, :, where].astype(F32) * (decay[i] * inv[i]) for i, h in enumerate(hs)]
        dot = [jnp.sum(grad[i] * out[i], 0, keepdims=True) for i in each]
        grad = [x.astype(BF16) for x in grad]
        for i, h in enumerate(hs):
            oh[h, where] = out[i].astype(BF16).T
        d_fq = [split_dot(dot_nn, state[i], grad[i]) - norm[i] * dot[i] for i in each]
        ds = [split_dot(dot_nt, feat[i], grad[i]) for i in each]
        gq = [split_dot(dot_nn, d_fq[i] * sigmoid(pre[i]), qx[h, where]) for i, h in enumerate(hs)]
        for i, h in enumerate(hs):
            dsb[j, h] = ds[i]
            dnb[j, h] = -spread(feat[i] * dot[i])
            slot = (h // per_group, lax.rem(h, per_group))
            if j == tiles:
                grads[slot] = gq[i]
            else:
                grads[slot] += gq[i]

    def put_out(n):
        return pltpu.make_async_copy(qin.at[at(n)], out_hbm.at[at(n)], out_sem.at[n])

    def write_out(n):
        qin[at(n)] = by_head(oh[:, at(n)])
        put_out(n).start()

    for j in range(tiles, 1, -1):
        over_heads(0, heads, UNROLL, lambda hs, j=j: combine(hs, j))

    def local_keys(hs):
        parts = [[] for _ in hs]
        for e in range(tiles):
            later = None
            if 0 < e < tiles - 1:
                later = [sum(dsb[j, h] for j in range(e + 2, tiles + 1)) for h in hs]
            near = [dsb[e + 1, h] for h in hs]
            kept = [(lane < count_before(h, e)).astype(F32) for h in hs]
            for i, h in enumerate(hs):
                values = vt[h, :, at(e)]
                if e == 0:
                    part = -kept[i] * (split_dot(dot_nn, near[i], values) + dnb[1, h])
                elif later is None:
                    part = (1.0 - kept[i]) * (split_dot(dot_nn, near[i], values) + dnb[e + 1, h])
                else:
                    both = split_dot(dot_nn, jnp.concatenate([near[i], later[i]], 0), values)
                    far = both[rank:] + sum(dnb[j, h] for j in range(e + 2, tiles + 1))
                    part = (1.0 - kept[i]) * (both[:rank] + dnb[e + 1, h]) + far
                parts[i].append(part * sigk[h, :, at(e)])
        for i, h in enumerate(hs):
            slot = (h // per_group, per_group + lax.rem(h, per_group))
            grads[slot] = split_dot(dot_nn, jnp.concatenate(parts[i], 1), kx[h, at(0, tiles)])

    def final_keys(hs):
        own = at(1, tiles)
        d_fk = [split_dot(dot_nn, gaf[h], vt[h, :, own]) + naf[h][:, :1] for h in hs]
        gk = [split_dot(dot_nn, d_fk[i] * sigk[h, :, own], kx[h, own]) for i, h in enumerate(hs)]
        for i, h in enumerate(hs):
            grads[h // per_group, per_group + lax.rem(h, per_group)] += gk[i]

    chunks = 2 * per_group
    owners, stride, per = owners_of(count, chunks)

    def owner_id(g, o):
        return o * stride + g % stride

    def is_owner(g):
        return lax.rem(flat, stride) == g % stride

    part = flat // stride

    def to_owner(g, o, sender):
        return pltpu.make_async_remote_copy(
            src_ref=grads.at[g, pl.ds(o * per, per)],
            dst_ref=gslots.at[g, sender],
            send_sem=red_out.at[g, o],
            recv_sem=red_in.at[g, sender],
            device_id=place(owner_id(g, o), axes),
            device_id_type=pl.DeviceIdType.MESH,
        )

    def to_all(g, o, target):
        return pltpu.make_async_remote_copy(
            src_ref=done.at[g, pl.ds(o * per, per)],
            dst_ref=done.at[g, pl.ds(o * per, per)],
            send_sem=back_out.at[g, target],
            recv_sem=back_in.at[g, o],
            device_id=place(target, axes),
            device_id_type=pl.DeviceIdType.MESH,
        )

    def over_owners(g, act):
        def step(i, carry):
            o = lax.rem(part + i, owners)

            @pl.when(owner_id(g, o) != flat)
            def _():
                act(o)

            return carry

        lax.fori_loop(0, owners, step, 0)

    def reduce_start(g):
        over_owners(g, lambda o: to_owner(g, o, flat).start())

    def reduce_own(g):
        @pl.when(is_owner(g))
        def _():
            def arrived(i, total):
                sender = lax.rem(flat + i, count)
                to_owner(g, part, sender).wait_recv()
                return total + gslots[g, sender]

            done[g, pl.ds(part * per, per)] = lax.fori_loop(1, count, arrived, grads[g, pl.ds(part * per, per)])

            def send(i, carry):
                to_all(g, part, lax.rem(flat + i, count)).start()
                return carry

            lax.fori_loop(1, count, send, 0)

    def reduce_end(g):
        over_owners(g, lambda o: to_all(g, o, lax.rem(flat + 1, count)).wait_recv())
        over_owners(g, lambda o: to_owner(g, o, flat).wait_send())

        @pl.when(is_owner(g))
        def _():
            def sent(i, carry):
                to_all(g, part, lax.rem(flat + i, count)).wait_send()
                return carry

            lax.fori_loop(1, count, sent, 0)

        for i in range(per_group):
            gq_ref[g * per_group + i] = done[g, i]
            gk_ref[g * per_group + i] = done[g, per_group + i]

    for n in range(1, tiles):
        write_out(n)

    for g in range(GROUPS):
        @pl.when(me > 0)
        def _(g=g):
            halo_copy(g, 0).wait_recv()
            halo_copy(g, 1).wait_recv()

        group = slice(g * per_group, (g + 1) * per_group)
        kx[group, at(0)] = by_head(halo[g, 0])
        vx[group, at(0)] = by_head(halo[g, 1])

        def first_tile(hs):
            flip_values(hs, [0])
            key_states(hs, [0])
            sparse(hs, 1)
            combine(hs, 1)

        over_heads(g * per_group, (g + 1) * per_group, UNROLL, first_tile)
        every = range(1, tiles + 1)
        message_start(
            1, g, lambda h: sum(dsb[j, h] for j in every), lambda h: sum(dnb[j, h] for j in every)
        )
        over_heads(g * per_group, (g + 1) * per_group, UNROLL, local_keys)
    write_out(0)
    for g in range(GROUPS):
        message_sum(1, g, gaf, naf)
        over_heads(g * per_group, (g + 1) * per_group, UNROLL, final_keys)
        reduce_start(g)
    for g in range(GROUPS):
        reduce_own(g)
    for g in range(GROUPS):
        reduce_end(g)
    for g in range(GROUPS):
        @pl.when(me < peers - 1)
        def _(g=g):
            halo_copy(g, 0).wait_send()
            halo_copy(g, 1).wait_send()

        message_sent(0, g)
        message_sent(1, g)
    for n in range(tiles):
        put_out(n).wait()


def body(queries, keys, values, keep_count, query_map, key_map, cotangent):
    q_rows, k_rows, v_rows, cot = queries[0], keys[0], values[0], cotangent[0]
    tokens, heads, width = q_rows.shape
    rank = query_map.shape[2]
    tiles = tokens // TILE
    wq = jnp.swapaxes(query_map, 1, 2)
    wk = jnp.swapaxes(key_map, 1, 2)
    axes = ("seq", "batch")
    peers = lax.axis_size("seq")
    count = peers * lax.axis_size("batch")
    per_group = heads // GROUPS
    chunks = 2 * per_group
    owners, _, per = owners_of(count, chunks)
    block = (per_group + 2, rank, width)
    hbm = pl.BlockSpec(memory_space=pl.ANY)
    vmem = pl.BlockSpec(memory_space=pltpu.VMEM)
    smem = pl.BlockSpec(memory_space=pltpu.SMEM)
    dma = pltpu.SemaphoreType.DMA
    small = pltpu.VMEM((heads, rank, width), F32)
    tiled = pltpu.VMEM((tiles + 1, heads, rank, width), F32)
    out, gq, gk = pl.pallas_call(
        functools.partial(layer_kernel, "seq", axes),
        name="layer",
        in_specs=[smem, hbm, hbm, hbm, hbm, vmem, vmem],
        out_specs=[hbm, vmem, vmem],
        out_shape=[
            jax.ShapeDtypeStruct((tokens, heads, width), BF16),
            jax.ShapeDtypeStruct((heads, rank, width), F32),
            jax.ShapeDtypeStruct((heads, rank, width), F32),
        ],
        scratch_shapes=[pltpu.VMEM((tokens, heads, width), BF16)] * 4
        + [pltpu.VMEM((heads, tokens + TILE, width), BF16)] * 2
        + [
            pltpu.VMEM((heads, width, tokens + TILE), BF16),
            pltpu.VMEM((heads, tokens, width), BF16),
            pltpu.VMEM((heads, width, tokens), BF16),
            pltpu.VMEM((heads, tokens, width), BF16),
            pltpu.VMEM((GROUPS, 2, TILE, per_group, width), BF16),
            pltpu.VMEM((heads, width, tokens), F32),
            pltpu.VMEM((heads, 8, tokens), F32),
            pltpu.VMEM((heads, rank, tokens), F32),
            pltpu.VMEM((heads, rank, tokens + TILE), F32),
            tiled, tiled, tiled, tiled, small, small, tiled, tiled, small, small,
            pltpu.VMEM((2, GROUPS) + block, BF16),
            pltpu.VMEM((2, GROUPS, peers) + block, BF16),
            pltpu.VMEM((GROUPS, chunks, rank, width), F32),
            pltpu.VMEM((GROUPS, count, per, rank, width), F32),
            pltpu.VMEM((GROUPS, chunks, rank, width), F32),
            dma((4, tiles)), dma((GROUPS, 2)), dma((GROUPS, 2)), dma((2, GROUPS, peers)), dma((2, GROUPS, peers)),
            dma((GROUPS, owners)), dma((GROUPS, count)), dma((GROUPS, count)), dma((GROUPS, owners)), dma((tiles,)),
        ],
        compiler_params=pltpu.CompilerParams(
            collective_id=0, has_side_effects=True, vmem_limit_bytes=VMEM_LIMIT
        ),
    )(keep_count[0], q_rows, k_rows, v_rows, cot, wq, wk)
    return out[None], jnp.swapaxes(gq, 1, 2), jnp.swapaxes(gk, 1, 2)


def solution(mesh):
    placed = (
        P("batch", "seq", None, None),
        P("batch", "seq", None, None),
        P("batch", "seq", None, None),
        P("batch", None, None),
        P(),
        P(),
        P("batch", "seq", None, None),
    )
    return jax.shard_map(
        body,
        mesh=mesh,
        in_specs=placed,
        out_specs=(P("batch", "seq", None, None), P(), P()),
        check_vma=False,
    )
```

time: 98.6 us -> 65.2 us (0.66)
  Pallas kernels: 86.7 us -> 59.8 us
  starting transfers between devices: 4.97 us -> 0 us
    pallas_call x7 -> x1, Pallas kernels: 86.7 us -> 59.8 us  [body(): pl.pallas_call(functools.partial(layer_kernel, 'seq', axes), name='layer'...]
    ppermute x1 -> x0, starting transfers between devices: 4.97 us -> none  [body(): lax.ppermute(jnp.stack([k_rows[tokens - TILE:], v_rows[tokens - TILE:]]),...]
    slice x4 -> x0, local copies, waits for them, and re-layouts: 1.19 us -> none  [the longest x2 1.02 us: body(): k_rows[tokens - TILE:]]
    unnamed x4 -> x7, local copies, waits for them, and re-layouts: 3.9 us -> 4.57 us
  transfers between devices with their start and end apart: 1 -> 0, of which waited for: 0 -> 0; matrix products, arithmetic and copies ran while one was open for 1% -> 0% of each run, Pallas kernels for 40% -> 0%
where the time goes in v1:
time: 65.2 us; the launch traced here: 65 us
  Pallas kernels  59.8 us (92%)
  local copies, waits for them, and re-layouts  4.57 us (7%)
  between operations  0.66 us (1%)
    pallas_call x1, Pallas kernels, body(): pl.pallas_call(functools.partial(layer_kernel, 'seq', axes), name='layer'...  59.8 us
    unnamed x7, local copies, waits for them, and re-layouts  4.57 us

profile of v1, /device:TPU:0, one launch (start us, length us, event | category | flops | bytes accessed | tf_op | source)
XLA Modules:
  0.0 65.0 jit_solution(16434127873453375495)
XLA Ops:
  0.6 59.8 %layer.1 = (bf16[512,16,128]{2,1,0:T(8,128)(2,1)}, f32[16,8,128]{2,1,0:T(8,128)}, f32[16,8,128]{2,1,0:T(8,128)}) custom-call(s32[16,32]{1,0:T(8,128)} %bitcast.19, bf16[512,16,128]{2,1,0:T(8,128)(2,1)} %bitcast.10, bf16[512,16,128]{2,1,0:T(8,128)(2,1)} %bitcast.11, bf16[512,16,128]{2,1,0:T(8,128)(2,1)} %bitcast.12, bf16[512,16,128]{2,1,0:T(8,128)(2,1)} %bitcast.13, ...), custom_call_target="tpu_custom_call" | custom-call | tf_op jit(solution)/shard_map/layer/pallas_call | solution.py:518
  60.4 0.0 copy-start.1
  60.4 0.0 copy-start
  60.4 3.3 %copy.13 = bf16[1,512,16,128]{3,2,1,0:T(8,128)(2,1)} copy(bf16[1,512,16,128]{3,2,1,0:T(8,128)(2,1)} %bitcast.14) | data formatting | bytes 4194304
  63.7 0.0 copy-done.1
  63.7 0.6 copy.14
  64.4 0.0 copy-done
  64.4 0.6 copy.15
Async XLA Ops:
  60.4 3.3 %copy-start.1 = (f32[16,8,128]{2,1,0:T(8,128)S(1)}, f32[16,8,128]{2,1,0:T(8,128)}, u32[]{:S(2)}) copy-start(f32[16,8,128]{2,1,0:T(8,128)} %get-tuple-element.7) | copy-start | bytes 196612
  60.4 3.9 %copy-start = (f32[16,8,128]{2,1,0:T(8,128)S(1)}, f32[16,8,128]{2,1,0:T(8,128)}, u32[]{:S(2)}) copy-start(f32[16,8,128]{2,1,0:T(8,128)} %get-tuple-element.8) | copy-start | bytes 196612

commit v2 on v1

v2 whole, which is shorter than its diff:
```python
import functools
import math

import jax
import jax.numpy as jnp
from jax import lax
from jax.experimental import pallas as pl
from jax.experimental.pallas import tpu as pltpu
from jax.sharding import PartitionSpec as P

TILE = 128
SHIFT = 1.5
LOG2E = 1.0 / math.log(2.0)
MASKED = -1e30
F32 = jnp.float32
BF16 = jnp.bfloat16
GROUPS = 2
UNROLL = 4
EARLY_EVEN = 4
EARLY_ODD = 1
PIECES = 4
VMEM_LIMIT = 58 * 1024 * 1024


def dot_nt(a, b):
    return lax.dot_general(a, b, (((1,), (1,)), ((), ())), preferred_element_type=F32)


def dot_nn(a, b):
    return lax.dot_general(a, b, (((1,), (0,)), ((), ())), preferred_element_type=F32)


def dot_tn(a, b):
    return lax.dot_general(a, b, (((0,), (0,)), ((), ())), preferred_element_type=F32)


def by_head(x):
    return jnp.swapaxes(x, 0, 1)


def softplus(x):
    return jnp.maximum(x, 0.0) + jnp.log1p(jnp.exp(-jnp.abs(x)))


def sigmoid(x):
    return 1.0 / (1.0 + jnp.exp(-x))


def halves(x):
    top = x.astype(BF16)
    return top, (x - top.astype(F32)).astype(BF16)


def split_dot(dot, x, y):
    rows = x.shape[0]
    both = dot(jnp.concatenate(halves(x), 0), y)
    return both[:rows] + both[rows:]


def flat_id(axes):
    index, count = 0, 1
    for axis in axes:
        index = index * lax.axis_size(axis) + lax.axis_index(axis)
        count *= lax.axis_size(axis)
    return index, count


def place(flat, axes):
    where = {}
    for axis in reversed(axes):
        size = lax.axis_size(axis)
        where[axis] = lax.rem(flat, size)
        flat = flat // size
    return where


def greet(count, me, axes):
    barrier = pltpu.get_barrier_semaphore()

    def hello(i, carry):
        pl.semaphore_signal(
            barrier, inc=1, device_id=place(lax.rem(me + i, count), axes), device_id_type=pl.DeviceIdType.MESH
        )
        return carry

    lax.fori_loop(1, count, hello, 0)
    return barrier


def at(tile, count=1):
    return pl.ds(tile * TILE, count * TILE)


def owners_of(count, chunks):
    owners = min(count, chunks)
    return owners, chunks // owners


def layer_kernel(
    seq, axes, counts_hbm, q_hbm, k_hbm, v_hbm, c_hbm, wq_hbm, wk_hbm, out_ref, sums_ref,
    qin, kin, vin, cin, kx, vx, vt, qx, ct, oh, halo, num, rows, preq, sigk, sall, nall, skept, nkept,
    sin, nin, dsb, dnb, gaf, naf, counts_ref, wq_ref, wk_ref, prob, fkept,
    own, state_out, state_in, even_in, mine, slots, grads, gslots, done,
    in_sem, small_sem, halo_out, halo_in, pair_out, pair_in, even_out_sem, even_in_sem,
    msg_out, msg_in, red_out, red_in, back_out, back_in, out_sem,
):
    tokens, heads, width = q_hbm.shape
    rank = wq_hbm.shape[1]
    tiles = tokens // TILE
    per_group = heads // GROUPS
    factor = LOG2E / math.sqrt(width)
    me = lax.axis_index(seq)
    peers = lax.axis_size(seq)
    flat, count = flat_id(axes)
    sq = (seq,)
    barrier = greet(count, flat, axes)
    base = me * tiles
    lane = lax.broadcasted_iota(jnp.int32, (1, TILE), 1)
    sub = lax.broadcasted_iota(jnp.int32, (TILE, TILE), 0)
    causal = sub <= lax.broadcasted_iota(jnp.int32, (TILE, TILE), 1)

    pairs_in = [(k_hbm, kin), (v_hbm, vin), (q_hbm, qin), (c_hbm, cin)]
    loads = [pltpu.make_async_copy(hbm, vmem, in_sem.at[i]) for i, (hbm, vmem) in enumerate(pairs_in)]
    for copy in loads:
        copy.start()

    smalls = [
        pltpu.make_async_copy(counts_hbm, counts_ref, small_sem.at[0]),
        pltpu.make_async_copy(wk_hbm, wk_ref, small_sem.at[1]),
        pltpu.make_async_copy(wq_hbm, wq_ref, small_sem.at[2]),
    ]
    for copy in smalls:
        copy.start()

    @pl.when(me == 0)
    def _():
        halo[...] = jnp.zeros_like(halo)
        state_in[0] = jnp.zeros_like(state_in[0])

    even = lax.rem(me, 2) == 0
    half = TILE // 2
    pieces = [(g, i, r) for g in range(GROUPS) for i in range(2) for r in range(2)]

    def halo_copy(g, i, r):
        hbm = (k_hbm, v_hbm)[i]
        return pltpu.make_async_remote_copy(
            src_ref=hbm.at[pl.ds(tokens - TILE + r * half, half), pl.ds(g * per_group, per_group)],
            dst_ref=halo.at[g, i, pl.ds(r * half, half)],
            send_sem=halo_out,
            recv_sem=halo_in.at[g, i],
            device_id=place(lax.rem(me + 1, peers), sq),
            device_id_type=pl.DeviceIdType.MESH,
        )

    def whole_copy(ref, send_sem, recv_sem):
        return pltpu.make_async_remote_copy(
            src_ref=ref,
            dst_ref=ref,
            send_sem=send_sem,
            recv_sem=recv_sem,
            device_id=place(lax.rem(me + 1, peers), sq),
            device_id_type=pl.DeviceIdType.MESH,
        )

    def halo_wait(g, i):
        @pl.when(me > 0)
        def _():
            whole_copy(halo.at[g, i], halo_out, halo_in.at[g, i]).wait_recv()

    with jax.named_scope("barrier"):
        pl.semaphore_wait(barrier, count - 1)

    def halo_start(mine, some):
        @pl.when(mine & (me < peers - 1))
        def _():
            for piece in some:
                halo_copy(*piece).start()

    odd = jnp.logical_not(even)
    halo_start(even, pieces[:EARLY_EVEN])
    halo_start(odd, pieces[:EARLY_ODD])

    def count_before(h, e):
        if e:
            return counts_ref[h, base + e - 1]
        return jnp.where(me > 0, counts_ref[h, jnp.maximum(base - 1, 0)], 0)

    def pair_copy(i, target):
        return pltpu.make_async_remote_copy(
            src_ref=state_out.at[i],
            dst_ref=state_in.at[i],
            send_sem=pair_out.at[i],
            recv_sem=pair_in.at[i],
            device_id=place(target, sq),
            device_id_type=pl.DeviceIdType.MESH,
        )

    def even_copy(sender, target):
        return pltpu.make_async_remote_copy(
            src_ref=state_out.at[2],
            dst_ref=even_in.at[sender],
            send_sem=even_out_sem.at[target],
            recv_sem=even_in_sem.at[sender],
            device_id=place(2 * target, sq),
            device_id_type=pl.DeviceIdType.MESH,
        )

    def pack(i, total):
        state_out[i, :heads] = total[:heads].astype(BF16)
        state_out[i, heads], state_out[i, heads + 1] = halves(total[heads] + total[heads + 1])

    def set_states(total):
        norms = total[heads] + total[heads + 1]
        for h in range(heads):
            sin[h] = total[h]
            nin[h] = spread(jnp.where(lane == h, norms, 0.0))

    pair, pairs = me // 2, peers // 2

    def own_states():
        packed = jnp.zeros((rank, width), F32)
        for h in range(heads):
            own[h] = sum(sall[e, h] for e in ext)
            packed = jnp.where(lane == h, sum(nall[e, h] for e in ext), packed)
        own[heads] = packed
        own[heads + 1] = jnp.zeros((rank, width), F32)

        @pl.when(odd & (me < peers - 1))
        def _():
            pack(0, own[...])
            pair_copy(0, me + 1).start()

        halo_start(odd, pieces[EARLY_ODD:])

    def pair_states():
        @pl.when(even)
        def _():
            @pl.when(me > 0)
            def _():
                pair_copy(0, me + 1).wait_recv()

            pack(2, own[...] + state_in[0].astype(F32))

            def send(p, carry):
                even_copy(pair, p).start()
                return carry

            lax.fori_loop(pair + 1, pairs, send, 0)

    def even_states():
        @pl.when(even)
        def _():
            def received(p, total):
                even_copy(p, lax.rem(pair + 1, pairs)).wait_recv()
                return total + even_in[p].astype(F32)

            total = lax.fori_loop(0, pair, received, state_in[0].astype(F32))
            pack(1, own[...] + total)
            pair_copy(1, me + 1).start()

            halo_start(even, pieces[EARLY_EVEN:])
            set_states(total)

    def odd_states():
        @pl.when(odd)
        def _():
            pair_copy(1, me - 1).wait_recv()
            set_states(state_in[1].astype(F32))

    def states_sent():
        @pl.when(even)
        def _():
            def sent(p, carry):
                even_copy(pair, p).wait_send()
                return carry

            lax.fori_loop(pair + 1, pairs, sent, 0)
            pair_copy(1, me + 1).wait_send()

        @pl.when(odd & (me < peers - 1))
        def _():
            pair_copy(0, me + 1).wait_send()

    def message(g, sender, target):
        return pltpu.make_async_remote_copy(
            src_ref=mine.at[g],
            dst_ref=slots.at[g, sender],
            send_sem=msg_out.at[g, target],
            recv_sem=msg_in.at[g, sender],
            device_id=place(target, sq),
            device_id_type=pl.DeviceIdType.MESH,
        )

    def message_start(g):
        every = range(1, tiles + 1)
        packed = jnp.zeros((rank, width), F32)
        for i in range(per_group):
            h = g * per_group + i
            mine[g, i] = sum(dsb[j, h] for j in every).astype(BF16)
            packed = jnp.where(lane == i, sum(dnb[j, h] for j in every), packed)
        mine[g, per_group], mine[g, per_group + 1] = halves(packed)

        def send(p, carry):
            message(g, me, p).start()
            return carry

        lax.fori_loop(0, me, send, 0)

    def message_sent(g):
        def sent(p, carry):
            message(g, me, p).wait_send()
            return carry

        lax.fori_loop(0, me, sent, 0)

    def message_sum(g):
        def received(p, total):
            message(g, p, lax.rem(me + 1, peers)).wait_recv()
            return total + slots[g, p].astype(F32)

        total = lax.fori_loop(me + 1, peers, received, jnp.zeros((per_group + 2, rank, width), F32))
        norms = total[per_group] + total[per_group + 1]
        for i in range(per_group):
            gaf[g * per_group + i] = total[i]
            naf[g * per_group + i] = spread(jnp.where(lane == i, norms, 0.0))

    def spread(x):
        return jnp.broadcast_to(jnp.sum(x, 1, keepdims=True), (rank, width))

    def over_heads(first, last, step, act):
        def block(i, carry):
            act([first + i * step + u for u in range(step)])
            return carry

        lax.fori_loop(0, (last - first) // step, block, 0)

    ext = list(range(1, tiles + 1))
    with jax.named_scope("keys"):
        loads[0].wait()
        for n in range(tiles):
            kx[:, at(n + 1)] = by_head(kin[at(n)])
    with jax.named_scope("values"):
        loads[1].wait()
        for n in range(tiles):
            vx[:, at(n + 1)] = by_head(vin[at(n)])
    with jax.named_scope("maps"):
        for copy in smalls:
            copy.wait()

    def key_features(hs, tile_list):
        where = at(tile_list[0], len(tile_list))
        pre = [dot_nt(wk_ref[h], kx[h, where]) - SHIFT for h in hs]
        for h, p in zip(hs, pre):
            sigk[h, :, where] = sigmoid(p)
        return [softplus(p) for p in pre]

    def kept_part(hs, e, feat):
        return [f * (lane < count_before(h, e)).astype(F32) for f, h in zip(feat, hs)]

    def key_states(hs):
        feat = key_features(hs, ext)
        for e in ext:
            one = [f[:, (e - 1) * TILE : e * TILE] for f in feat]
            if e < tiles:
                kept = kept_part(hs, e, one)
                both = [split_dot(dot_nn, jnp.concatenate([o, k], 0), vx[h, at(e)]) for o, k, h in zip(one, kept, hs)]
                for i, h in enumerate(hs):
                    skept[e, h] = both[i][rank:]
                    nkept[e, h] = spread(kept[i])
            else:
                both = [split_dot(dot_nn, o, vx[h, at(e)]) for o, h in zip(one, hs)]
            for i, h in enumerate(hs):
                sall[e, h] = both[i][:rank]
                nall[e, h] = spread(one[i])

    with jax.named_scope("states"):
        over_heads(0, heads, UNROLL, key_states)
        own_states()

    def flip_values(hs, tile_list):
        for h in hs:
            for e in tile_list:
                vt[h, :, at(e)] = vx[h, at(e)].T

    with jax.named_scope("flip_v"):
        over_heads(0, heads, UNROLL, lambda hs: flip_values(hs, ext))
    with jax.named_scope("queries"):
        loads[2].wait()
        for n in range(tiles):
            qx[:, at(n)] = by_head(qin[at(n)])

    def query_features(hs):
        pre = [dot_nt(wq_ref[h], qx[h]) - SHIFT for h in hs]
        for h, p in zip(hs, pre):
            preq[h] = p

    with jax.named_scope("qfeat"):
        over_heads(0, heads, UNROLL, query_features)
    def weights(hs, j):
        each = range(len(hs))
        scores = [dot_nt(kx[h, at(j - 1, 2)], qx[h, at(j - 1)]) for h in hs]
        old = [jnp.where(sub < count_before(h, j - 1), scores[i][:TILE], MASKED) for i, h in enumerate(hs)]
        new = [jnp.where(causal, scores[i][TILE:], MASKED) for i in each]
        top = [jnp.max(jnp.maximum(old[i], new[i]), 0, keepdims=True) * factor for i in each]
        old = [jnp.exp2(old[i] * factor - top[i]) for i in each]
        new = [jnp.exp2(new[i] * factor - top[i]) for i in each]
        for i, h in enumerate(hs):
            rows[h, 0:1, at(j - 1)] = jnp.sum(old[i] + new[i], 0, keepdims=True)
            rows[h, 1:2, at(j - 1)] = top[i]
        return [jnp.concatenate([old[i].astype(BF16), new[i].astype(BF16)], 0) for i in each]

    def weighted(hs, j, weight):
        numer = [dot_nn(vt[h, :, at(j - 1, 2)], w) for h, w in zip(hs, weight)]
        for h, x in zip(hs, numer):
            num[h, :, at(j - 1)] = x

    def sparse(hs, j):
        weighted(hs, j, weights(hs, j))

    with jax.named_scope("sparse"):
        for j in range(2, tiles + 1):
            over_heads(0, heads, UNROLL, lambda hs, j=j: sparse(hs, j))
            if j == 2:
                with jax.named_scope("pair_states"):
                    pair_states()
    with jax.named_scope("even_states"):
        even_states()
    with jax.named_scope("cot"):
        loads[3].wait()
        for n in range(tiles):
            oh[:, at(n)] = by_head(cin[at(n)])

    def flip_cotangent(hs):
        for h in hs:
            for n in range(tiles):
                ct[h, :, at(n)] = oh[h, at(n)].T

    with jax.named_scope("flip_c"):
        over_heads(0, heads, UNROLL, flip_cotangent)
    with jax.named_scope("odd_states"):
        odd_states()

    def combine(hs, j):
        each = range(len(hs))
        where = at(j - 1)
        pre = [preq[h, :, where] for h in hs]
        feat = [softplus(p) for p in pre]
        state = [sum([sall[e, h] for e in range(1, j)], sin[h]) - skept[j - 1, h] for h in hs]
        norm = [sum([nall[e, h] for e in range(1, j)], nin[h]) - nkept[j - 1, h] for h in hs]
        decay = [jnp.exp2(-rows[h, 1:2, where]) for h in hs]
        kernel = []
        for i in each:
            fq_top, fq_low = halves(feat[i])
            st_top, st_low = halves(state[i])
            kernel.append(
                dot_tn(jnp.concatenate([st_top, st_top, st_low], 0), jnp.concatenate([fq_top, fq_low, fq_top], 0))
            )
        den = [jnp.sum(norm[i] * feat[i], 0, keepdims=True) for i in each]
        inv = [1.0 / (rows[h, 0:1, where] + decay[i] * den[i]) for i, h in enumerate(hs)]
        out = [(num[h, :, where] + decay[i] * kernel[i]) * inv[i] for i, h in enumerate(hs)]
        grad = [ct[h, :, where].astype(F32) * (decay[i] * inv[i]) for i, h in enumerate(hs)]
        dot = [jnp.sum(grad[i] * out[i], 0, keepdims=True) for i in each]
        grad = [x.astype(BF16) for x in grad]
        for i, h in enumerate(hs):
            oh[h, where] = out[i].astype(BF16).T
        d_fq = [split_dot(dot_nn, state[i], grad[i]) - norm[i] * dot[i] for i in each]
        ds = [split_dot(dot_nt, feat[i], grad[i]) for i in each]
        gq = [split_dot(dot_nn, d_fq[i] * sigmoid(pre[i]), qx[h, where]) for i, h in enumerate(hs)]
        for i, h in enumerate(hs):
            dsb[j, h] = ds[i]
            dnb[j, h] = -spread(feat[i] * dot[i])
            slot = (h // per_group, lax.rem(h, per_group))
            if j == tiles:
                grads[slot] = gq[i]
            else:
                grads[slot] += gq[i]

    with jax.named_scope("combine"):
        for j in range(tiles, 1, -1):
            over_heads(0, heads, UNROLL, lambda hs, j=j: combine(hs, j))

    def local_keys(hs):
        parts = [[] for _ in hs]
        for e in range(tiles):
            later = None
            if 0 < e < tiles - 1:
                later = [sum(dsb[j, h] for j in range(e + 2, tiles + 1)) for h in hs]
            near = [dsb[e + 1, h] for h in hs]
            kept = [(lane < count_before(h, e)).astype(F32) for h in hs]
            for i, h in enumerate(hs):
                values = vt[h, :, at(e)]
                if e == 0:
                    part = -kept[i] * (split_dot(dot_nn, near[i], values) + dnb[1, h])
                elif later is None:
                    part = (1.0 - kept[i]) * (split_dot(dot_nn, near[i], values) + dnb[e + 1, h])
                else:
                    both = split_dot(dot_nn, jnp.concatenate([near[i], later[i]], 0), values)
                    far = both[rank:] + sum(dnb[j, h] for j in range(e + 2, tiles + 1))
                    part = (1.0 - kept[i]) * (both[:rank] + dnb[e + 1, h]) + far
                parts[i].append(part * sigk[h, :, at(e)])
        for i, h in enumerate(hs):
            slot = (h // per_group, per_group + lax.rem(h, per_group))
            grads[slot] = split_dot(dot_nn, jnp.concatenate(parts[i], 1), kx[h, at(0, tiles)])

    def final_keys(hs):
        own = at(1, tiles)
        d_fk = [split_dot(dot_nn, gaf[h], vt[h, :, own]) + naf[h][:, :1] for h in hs]
        gk = [split_dot(dot_nn, d_fk[i] * sigk[h, :, own], kx[h, own]) for i, h in enumerate(hs)]
        for i, h in enumerate(hs):
            grads[h // per_group, per_group + lax.rem(h, per_group)] += gk[i]

    chunks = 2 * per_group
    owners, per = owners_of(count, chunks)

    def owner_id(g, o):
        return middle + o

    def is_owner(g):
        return (flat >= middle) & (flat < middle + owners)

    middle = (count - owners) // 2
    part = lax.rem(flat - middle + count, owners)

    def to_owner(g, o, sender):
        return pltpu.make_async_remote_copy(
            src_ref=grads.at[g, pl.ds(o * per, per)],
            dst_ref=gslots.at[g, lax.rem(sender - owner_id(g, o) + count - 1, count)],
            send_sem=red_out.at[g],
            recv_sem=red_in.at[g],
            device_id=place(owner_id(g, o), axes),
            device_id_type=pl.DeviceIdType.MESH,
        )

    def to_all(g, o, target):
        return pltpu.make_async_remote_copy(
            src_ref=done.at[g, pl.ds(o * per, per)],
            dst_ref=done.at[g, pl.ds(o * per, per)],
            send_sem=back_out.at[g],
            recv_sem=back_in.at[g],
            device_id=place(target, axes),
            device_id_type=pl.DeviceIdType.MESH,
        )

    def over_owners(g, act):
        def step(i, carry):
            o = lax.rem(part + i, owners)

            @pl.when(owner_id(g, o) != flat)
            def _():
                act(o)

            return carry

        lax.fori_loop(0, owners, step, 0)

    def reduce_start(g):
        over_owners(g, lambda o: to_owner(g, o, flat).start())

    def reduce_own(g):
        @pl.when(is_owner(g))
        def _():
            whole_copy(gslots.at[g], red_out.at[g], red_in.at[g]).wait_recv()
            mine_now = pl.ds(part * per, per)
            done[g, mine_now] = lax.fori_loop(0, count - 1, lambda i, t: t + gslots[g, i], grads[g, mine_now])

            def send(i, carry):
                to_all(g, part, lax.rem(flat + i, count)).start()
                return carry

            lax.fori_loop(1, count, send, 0)

    def reduce_end(g):
        @pl.when(is_owner(g))
        def _():
            others = pl.ds(0, chunks - per)
            whole_copy(done.at[g, others], back_out.at[g], back_in.at[g]).wait_recv()
            whole_copy(grads.at[g, others], red_out.at[g], red_in.at[g]).wait_send()
            whole_copy(gslots.at[g], back_out.at[g], back_in.at[g]).wait_send()

        @pl.when(jnp.logical_not(is_owner(g)))
        def _():
            whole_copy(done.at[g], back_out.at[g], back_in.at[g]).wait_recv()
            whole_copy(grads.at[g], red_out.at[g], red_in.at[g]).wait_send()

        for i in range(per_group):
            sums_ref[g * per_group + i] = done[g, i]
            sums_ref[heads + g * per_group + i] = done[g, per_group + i]

    put_out = pltpu.make_async_copy(qin, out_ref, out_sem)

    def write_out(n):
        qin[at(n)] = by_head(oh[:, at(n)])

    with jax.named_scope("write_out"):
        for n in range(1, tiles):
            write_out(n)

    def first_keys(hs):
        kept = kept_part(hs, 0, key_features(hs, [0]))
        weight = weights(hs, 1)
        for i, h in enumerate(hs):
            fkept[h] = kept[i]
            prob[h] = weight[i]

    def first_values(hs):
        flip_values(hs, [0])
        kept = [fkept[h] for h in hs]
        state = [split_dot(dot_nn, k, vx[h, at(0)]) for k, h in zip(kept, hs)]
        for i, h in enumerate(hs):
            skept[0, h] = state[i]
            nkept[0, h] = spread(kept[i])
        weighted(hs, 1, [prob[h] for h in hs])
        combine(hs, 1)

    for g in range(GROUPS):
        first, last = g * per_group, (g + 1) * per_group
        with jax.named_scope("halo_k"):
            halo_wait(g, 0)
        with jax.named_scope("first_keys"):
            kx[first:last, at(0)] = by_head(halo[g, 0])
            over_heads(first, last, UNROLL, first_keys)
        with jax.named_scope("halo_v"):
            halo_wait(g, 1)
        with jax.named_scope("first_values"):
            vx[first:last, at(0)] = by_head(halo[g, 1])
            over_heads(first, last, UNROLL, first_values)
        with jax.named_scope("send_ds"):
            message_start(g)
        with jax.named_scope("local_keys"):
            over_heads(first, last, UNROLL, local_keys)
    with jax.named_scope("write_0"):
        write_out(0)
        put_out.start()
    for g in range(GROUPS):
        with jax.named_scope("wait_ds"):
            message_sum(g)
        with jax.named_scope("final_keys"):
            over_heads(g * per_group, (g + 1) * per_group, UNROLL, final_keys)
        with jax.named_scope("red_start"):
            reduce_start(g)
    with jax.named_scope("red_own"):
        for g in range(GROUPS):
            reduce_own(g)
    with jax.named_scope("red_end"):
        for g in range(GROUPS):
            reduce_end(g)
    with jax.named_scope("sent"):
        @pl.when(me < peers - 1)
        def _():
            whole_copy(halo, halo_out, halo_in.at[0, 0]).wait_send()

        states_sent()
        for g in range(GROUPS):
            message_sent(g)
        put_out.wait()


def finish_kernel(rows_hbm, sums_hbm, out_hbm, gq_hbm, gk_hbm, rows, sums, in_sem, out_sem):
    tokens = rows.shape[0]
    heads = gq_hbm.shape[0]
    parts = [pl.ds(i * heads, heads) for i in range(2)]
    sums_in = pltpu.make_async_copy(sums_hbm, sums, in_sem.at[PIECES])
    chunks = [pl.ds(i * (tokens // PIECES), tokens // PIECES) for i in range(PIECES)]
    rows_in = [pltpu.make_async_copy(rows_hbm.at[c], rows.at[c], in_sem.at[i]) for i, c in enumerate(chunks)]
    rows_out = [pltpu.make_async_copy(rows.at[c], out_hbm.at[c], out_sem.at[i]) for i, c in enumerate(chunks)]
    outs = [(sums.at[parts[0]], gq_hbm), (sums.at[parts[1]], gk_hbm)]
    sums_out = [pltpu.make_async_copy(a, b, out_sem.at[PIECES + i]) for i, (a, b) in enumerate(outs)]
    sums_in.start()
    for copy in rows_in:
        copy.start()
    sums_in.wait()
    for copy in sums_out:
        copy.start()
    for i in range(PIECES):
        rows_in[i].wait()
        rows_out[i].start()
    for copy in sums_out + rows_out:
        copy.wait()


def body(queries, keys, values, keep_count, query_map, key_map, cotangent):
    q_rows, k_rows, v_rows, cot = queries[0], keys[0], values[0], cotangent[0]
    tokens, heads, width = q_rows.shape
    rank = query_map.shape[2]
    tiles = tokens // TILE
    axes = ("seq", "batch")
    peers = lax.axis_size("seq")
    count = peers * lax.axis_size("batch")
    per_group = heads // GROUPS
    chunks = 2 * per_group
    owners, per = owners_of(count, chunks)
    block = (per_group + 2, rank, width)
    hbm = pl.BlockSpec(memory_space=pltpu.HBM)
    vmem = pl.BlockSpec(memory_space=pltpu.VMEM)
    dma = pltpu.SemaphoreType.DMA
    small = pltpu.VMEM((heads, rank, width), F32)
    tiled = pltpu.VMEM((tiles + 1, heads, rank, width), F32)
    states = (heads + 2, rank, width)
    packed = pltpu.VMEM((heads, rank, width), BF16)
    operands = [q_rows, k_rows, v_rows, cot, jnp.swapaxes(query_map, 1, 2), jnp.swapaxes(key_map, 1, 2)]
    rows, sums = pl.pallas_call(
        functools.partial(layer_kernel, "seq", axes),
        name="layer",
        in_specs=[hbm] * 7,
        out_specs=[hbm, vmem],
        out_shape=[
            jax.ShapeDtypeStruct((tokens, heads, width), BF16),
            jax.ShapeDtypeStruct((2 * heads, rank, width), F32),
        ],
        scratch_shapes=[pltpu.VMEM((tokens, heads, width), BF16)] * 4
        + [pltpu.VMEM((heads, tokens + TILE, width), BF16)] * 2
        + [
            pltpu.VMEM((heads, width, tokens + TILE), BF16),
            pltpu.VMEM((heads, tokens, width), BF16),
            pltpu.VMEM((heads, width, tokens), BF16),
            pltpu.VMEM((heads, tokens, width), BF16),
            pltpu.VMEM((GROUPS, 2, TILE, per_group, width), BF16),
            pltpu.VMEM((heads, width, tokens), F32),
            pltpu.VMEM((heads, 8, tokens), F32),
            pltpu.VMEM((heads, rank, tokens), F32),
            pltpu.VMEM((heads, rank, tokens + TILE), F32),
            tiled, tiled, tiled, tiled, small, small, tiled, tiled, small, small,
            pltpu.SMEM(keep_count.shape[1:], jnp.int32),
            packed, packed,
            pltpu.VMEM((heads, 2 * TILE, TILE), BF16),
            small,
            pltpu.VMEM(states, F32),
            pltpu.VMEM((3,) + states, BF16),
            pltpu.VMEM((2,) + states, BF16),
            pltpu.VMEM((peers // 2,) + states, BF16),
            pltpu.VMEM((GROUPS,) + block, BF16),
            pltpu.VMEM((GROUPS, peers) + block, BF16),
            pltpu.VMEM((GROUPS, chunks, rank, width), F32),
            pltpu.VMEM((GROUPS, count - 1, per, rank, width), F32),
            pltpu.VMEM((GROUPS, chunks, rank, width), F32),
            dma((4,)), dma((3,)), dma(()), dma((GROUPS, 2)), dma((2,)), dma((2,)),
            dma((peers // 2,)), dma((peers // 2,)), dma((GROUPS, peers)), dma((GROUPS, peers)),
            dma((GROUPS,)), dma((GROUPS,)), dma((GROUPS,)), dma((GROUPS,)), dma(()),
        ],
        compiler_params=pltpu.CompilerParams(
            collective_id=0, has_side_effects=True, vmem_limit_bytes=VMEM_LIMIT
        ),
    )(keep_count[0], *operands)
    out, gq, gk = pl.pallas_call(
        finish_kernel,
        name="finish",
        in_specs=[hbm, hbm],
        out_specs=[hbm, hbm, hbm],
        out_shape=[
            jax.ShapeDtypeStruct((tokens, heads, width), BF16),
            jax.ShapeDtypeStruct((heads, rank, width), F32),
            jax.ShapeDtypeStruct((heads, rank, width), F32),
        ],
        scratch_shapes=[
            pltpu.VMEM((tokens, heads, width), BF16),
            pltpu.VMEM((2 * heads, rank, width), F32),
            dma((PIECES + 1,)), dma((PIECES + 2,)),
        ],
        compiler_params=pltpu.CompilerParams(vmem_limit_bytes=VMEM_LIMIT),
    )(rows, sums)
    return out[None], jnp.swapaxes(gq, 1, 2), jnp.swapaxes(gk, 1, 2)


def solution(mesh):
    placed = (
        P("batch", "seq", None, None),
        P("batch", "seq", None, None),
        P("batch", "seq", None, None),
        P("batch", None, None),
        P(),
        P(),
        P("batch", "seq", None, None),
    )
    return jax.shard_map(
        body,
        mesh=mesh,
        in_specs=placed,
        out_specs=(P("batch", "seq", None, None), P(), P()),
        check_vma=False,
    )
```

time: 65.2 us -> 54.2 us (0.83)
  Pallas kernels: 59.8 us -> 53.4 us
  local copies, waits for them, and re-layouts: 4.57 us -> 0 us
    pallas_call x1, Pallas kernels: 59.8 us -> 50.9 us  [body(): pl.pallas_call(functools.partial(layer_kernel, 'seq', axes), name='layer'...]
    unnamed x7 -> x0, local copies, waits for them, and re-layouts: 4.57 us -> none
    pallas_call x0 -> x1, Pallas kernels: none -> 2.52 us  [body(): pl.pallas_call(finish_kernel, name='finish', in_specs=[hbm, hbm], out_spe...]
where the time goes in v2:
time: 54.2 us; the launch traced here: 54.1 us
  Pallas kernels  53.4 us (99%)
  between operations  0.64 us (1%)
    pallas_call x1, Pallas kernels, body(): pl.pallas_call(functools.partial(layer_kernel, 'seq', axes), name='layer'...  50.9 us
    pallas_call x1, Pallas kernels, body(): pl.pallas_call(finish_kernel, name='finish', in_specs=[hbm, hbm], out_spe...  2.52 us

profile of v2, /device:TPU:0, one launch (start us, length us, event | category | flops | bytes accessed | tf_op | source)
XLA Modules:
  0.0 54.1 jit_solution(4594109454304961214)
XLA Ops:
  0.6 50.9 %layer.1 = (bf16[512,16,128]{2,1,0:T(8,128)(2,1)}, f32[32,8,128]{2,1,0:T(8,128)}) custom-call(s32[16,32]{1,0:T(8,128)} %bitcast.16, bf16[512,16,128]{2,1,0:T(8,128)(2,1)} %bitcast.10, bf16[512,16,128]{2,1,0:T(8,128)(2,1)} %bitcast.11, bf16[512,16,128]{2,1,0:T(8,128)(2,1)} %bitcast.12, bf16[512,16,128]{2,1,0:T(8,128)(2,1)} %bitcast.13, ...), custom_call_target="tpu_custom_call" | custom-call | tf_op jit(solution)/shard_map/layer/pallas_call | solution.py:701
  51.5 2.5 %finish.1 = (bf16[512,16,128]{2,1,0:T(8,128)(2,1)}, f32[16,8,128]{2,1,0:T(8,128)}, f32[16,8,128]{2,1,0:T(8,128)}) custom-call(bf16[512,16,128]{2,1,0:T(8,128)(2,1)} %get-tuple-element.8.rows_hbm, f32[32,8,128]{2,1,0:T(8,128)} %get-tuple-element.9.sums_hbm), custom_call_target="tpu_custom_call" | custom-call | tf_op jit(solution)/shard_map/finish/pallas_call | solution.py:744

commit v3 on v2

--- a/solution.py
+++ b/solution.py
@@ -16,10 +16,12 @@
 BF16 = jnp.bfloat16
 GROUPS = 2
 UNROLL = 4
-EARLY_EVEN = 4
-EARLY_ODD = 1
-PIECES = 4
-VMEM_LIMIT = 58 * 1024 * 1024
+CUTS = 4
+EARLY_EVEN = 9
+EARLY_ODD = 3
+LATE = 8
+PARTS = 4
+VMEM_LIMIT = 50 * 1024 * 1024
 
 
 def dot_nt(a, b):
@@ -74,16 +76,32 @@
     return where
 
 
-def greet(count, me, axes):
+def each_other(axes, act):
+    outer, inner = axes
+    me, mine = lax.axis_index(outer), lax.axis_index(inner)
+    peers, others = lax.axis_size(outer), lax.axis_size(inner)
+
+    def far(i, carry):
+        s = me + i
+        s = jnp.where(s >= peers, s - peers, s)
+        for b in range(others):
+            act({outer: s, inner: b})
+        return carry
+
+    lax.fori_loop(1, peers, far, 0)
+    for b in range(others):
+
+        @pl.when(mine != b)
+        def _(b=b):
+            act({outer: me, inner: b})
+
+
+def greet(axes):
     barrier = pltpu.get_barrier_semaphore()
-
-    def hello(i, carry):
-        pl.semaphore_signal(
-            barrier, inc=1, device_id=place(lax.rem(me + i, count), axes), device_id_type=pl.DeviceIdType.MESH
-        )
-        return carry
-
-    lax.fori_loop(1, count, hello, 0)
+    each_other(
+        axes,
+        lambda where: pl.semaphore_signal(barrier, inc=1, device_id=where, device_id_type=pl.DeviceIdType.MESH),
+    )
     return barrier
 
 
@@ -93,16 +111,17 @@
 
 def owners_of(count, chunks):
     owners = min(count, chunks)
-    return owners, chunks // owners
+    stride = 2 if count >= 2 * owners else 1
+    return owners, stride, (count - owners * stride) // 2 + stride - 1
 
 
 def layer_kernel(
     seq, axes, counts_hbm, q_hbm, k_hbm, v_hbm, c_hbm, wq_hbm, wk_hbm, out_ref, sums_ref,
     qin, kin, vin, cin, kx, vx, vt, qx, ct, oh, halo, num, rows, preq, sigk, sall, nall, skept, nkept,
-    sin, nin, dsb, dnb, gaf, naf, counts_ref, wq_ref, wk_ref, prob, fkept,
-    own, state_out, state_in, even_in, mine, slots, grads, gslots, done,
-    in_sem, small_sem, halo_out, halo_in, pair_out, pair_in, even_out_sem, even_in_sem,
-    msg_out, msg_in, red_out, red_in, back_out, back_in, out_sem,
+    sin, nin, dsb, dnb, gaf, naf, counts_ref, wq_ref, wk_ref, prob, fkept, sent_halo,
+    own, state_out, state_in, even_in, mine, slots, grads, qslots, kslots, done,
+    in_sem, edge_sem, small_sem, halo_out, halo_in, pair_out, pair_in, even_out_sem, even_in_sem,
+    msg_out, msg_in, red_out, red_in, back_out, back_in,
 ):
     tokens, heads, width = q_hbm.shape
     rank = wq_hbm.shape[1]
@@ -113,12 +132,21 @@
     peers = lax.axis_size(seq)
     flat, count = flat_id(axes)
     sq = (seq,)
-    barrier = greet(count, flat, axes)
+    barrier = greet(axes)
     base = me * tiles
     lane = lax.broadcasted_iota(jnp.int32, (1, TILE), 1)
     sub = lax.broadcasted_iota(jnp.int32, (TILE, TILE), 0)
     causal = sub <= lax.broadcasted_iota(jnp.int32, (TILE, TILE), 1)
 
+    early = [
+        pltpu.make_async_copy(
+            hbm.at[pl.ds(tokens - TILE, TILE), pl.ds(g * per_group, per_group)], sent_halo.at[g, i], edge_sem.at[g, i]
+        )
+        for g in range(GROUPS)
+        for i, hbm in enumerate((k_hbm, v_hbm))
+    ]
+    for copy in early:
+        copy.start()
     pairs_in = [(k_hbm, kin), (v_hbm, vin), (q_hbm, qin), (c_hbm, cin)]
     loads = [pltpu.make_async_copy(hbm, vmem, in_sem.at[i]) for i, (hbm, vmem) in enumerate(pairs_in)]
     for copy in loads:
@@ -138,14 +166,13 @@
         state_in[0] = jnp.zeros_like(state_in[0])
 
     even = lax.rem(me, 2) == 0
-    half = TILE // 2
-    pieces = [(g, i, r) for g in range(GROUPS) for i in range(2) for r in range(2)]
+    cut = TILE // CUTS
+    pieces = [(g, i, r) for g in range(GROUPS) for i in range(2) for r in range(CUTS)]
 
     def halo_copy(g, i, r):
-        hbm = (k_hbm, v_hbm)[i]
         return pltpu.make_async_remote_copy(
-            src_ref=hbm.at[pl.ds(tokens - TILE + r * half, half), pl.ds(g * per_group, per_group)],
-            dst_ref=halo.at[g, i, pl.ds(r * half, half)],
+            src_ref=sent_halo.at[g, i, pl.ds(r * cut, cut)],
+            dst_ref=halo.at[g, i, pl.ds(r * cut, cut)],
             send_sem=halo_out,
             recv_sem=halo_in.at[g, i],
             device_id=place(lax.rem(me + 1, peers), sq),
@@ -167,6 +194,8 @@
         def _():
             whole_copy(halo.at[g, i], halo_out, halo_in.at[g, i]).wait_recv()
 
+    for copy in early[:2]:
+        copy.wait()
     with jax.named_scope("barrier"):
         pl.semaphore_wait(barrier, count - 1)
 
@@ -177,8 +206,12 @@
                 halo_copy(*piece).start()
 
     odd = jnp.logical_not(even)
-    halo_start(even, pieces[:EARLY_EVEN])
+    first_group = 2 * CUTS
+    halo_start(even, pieces[:first_group])
     halo_start(odd, pieces[:EARLY_ODD])
+    for copy in early[2:]:
+        copy.wait()
+    halo_start(even, pieces[first_group:EARLY_EVEN])
 
     def count_before(h, e):
         if e:
@@ -469,11 +502,10 @@
         for i, h in enumerate(hs):
             dsb[j, h] = ds[i]
             dnb[j, h] = -spread(feat[i] * dot[i])
-            slot = (h // per_group, lax.rem(h, per_group))
             if j == tiles:
-                grads[slot] = gq[i]
+                grads[h] = gq[i]
             else:
-                grads[slot] += gq[i]
+                grads[h] += gq[i]
 
     with jax.named_scope("combine"):
         for j in range(tiles, 1, -1):
@@ -499,97 +531,86 @@
                     part = (1.0 - kept[i]) * (both[:rank] + dnb[e + 1, h]) + far
                 parts[i].append(part * sigk[h, :, at(e)])
         for i, h in enumerate(hs):
-            slot = (h // per_group, per_group + lax.rem(h, per_group))
-            grads[slot] = split_dot(dot_nn, jnp.concatenate(parts[i], 1), kx[h, at(0, tiles)])
+            grads[heads + h] = split_dot(dot_nn, jnp.concatenate(parts[i], 1), kx[h, at(0, tiles)])
 
     def final_keys(hs):
         own = at(1, tiles)
         d_fk = [split_dot(dot_nn, gaf[h], vt[h, :, own]) + naf[h][:, :1] for h in hs]
         gk = [split_dot(dot_nn, d_fk[i] * sigk[h, :, own], kx[h, own]) for i, h in enumerate(hs)]
         for i, h in enumerate(hs):
-            grads[h // per_group, per_group + lax.rem(h, per_group)] += gk[i]
-
-    chunks = 2 * per_group
-    owners, per = owners_of(count, chunks)
-
-    def owner_id(g, o):
-        return middle + o
-
-    def is_owner(g):
-        return (flat >= middle) & (flat < middle + owners)
-
-    middle = (count - owners) // 2
-    part = lax.rem(flat - middle + count, owners)
-
-    def to_owner(g, o, sender):
+            grads[heads + h] += gk[i]
+
+    owners, stride, middle = owners_of(count, per_group)
+    rounds = [(0, heads)] + [(heads + g * per_group, per_group) for g in range(GROUPS)]
+    ahead = flat - middle + count * stride
+    part = lax.rem(ahead // stride, owners)
+    inside = (flat >= middle) & (flat < middle + owners * stride) & (lax.rem(ahead, stride) == 0)
+
+    def share(r, o):
+        first, size = rounds[r]
+        per = size // owners
+        return pl.ds(first + o * per, per)
+
+    def arriving(r):
+        return kslots.at[r - 1] if r else qslots
+
+    def to_owner(r, o):
+        target = middle + o * stride
         return pltpu.make_async_remote_copy(
-            src_ref=grads.at[g, pl.ds(o * per, per)],
-            dst_ref=gslots.at[g, lax.rem(sender - owner_id(g, o) + count - 1, count)],
-            send_sem=red_out.at[g],
-            recv_sem=red_in.at[g],
-            device_id=place(owner_id(g, o), axes),
+            src_ref=grads.at[share(r, o)],
+            dst_ref=arriving(r).at[lax.rem(flat - target + count - 1, count)],
+            send_sem=red_out.at[r],
+            recv_sem=red_in.at[r],
+            device_id=dict(zip(axes, divmod(target, lax.axis_size(axes[1])))),
             device_id_type=pl.DeviceIdType.MESH,
         )
 
-    def to_all(g, o, target):
+    def to_all(r, where):
         return pltpu.make_async_remote_copy(
-            src_ref=done.at[g, pl.ds(o * per, per)],
-            dst_ref=done.at[g, pl.ds(o * per, per)],
-            send_sem=back_out.at[g],
-            recv_sem=back_in.at[g],
-            device_id=place(target, axes),
+            src_ref=done.at[share(r, part)],
+            dst_ref=done.at[share(r, part)],
+            send_sem=back_out.at[r],
+            recv_sem=back_in.at[r],
+            device_id=where,
             device_id_type=pl.DeviceIdType.MESH,
         )
 
-    def over_owners(g, act):
-        def step(i, carry):
-            o = lax.rem(part + i, owners)
-
-            @pl.when(owner_id(g, o) != flat)
-            def _():
-                act(o)
-
-            return carry
-
-        lax.fori_loop(0, owners, step, 0)
-
-    def reduce_start(g):
-        over_owners(g, lambda o: to_owner(g, o, flat).start())
-
-    def reduce_own(g):
-        @pl.when(is_owner(g))
-        def _():
-            whole_copy(gslots.at[g], red_out.at[g], red_in.at[g]).wait_recv()
-            mine_now = pl.ds(part * per, per)
-            done[g, mine_now] = lax.fori_loop(0, count - 1, lambda i, t: t + gslots[g, i], grads[g, mine_now])
-
-            def send(i, carry):
-                to_all(g, part, lax.rem(flat + i, count)).start()
-                return carry
-
-            lax.fori_loop(1, count, send, 0)
-
-    def reduce_end(g):
-        @pl.when(is_owner(g))
-        def _():
-            others = pl.ds(0, chunks - per)
-            whole_copy(done.at[g, others], back_out.at[g], back_in.at[g]).wait_recv()
-            whole_copy(grads.at[g, others], red_out.at[g], red_in.at[g]).wait_send()
-            whole_copy(gslots.at[g], back_out.at[g], back_in.at[g]).wait_send()
-
-        @pl.when(jnp.logical_not(is_owner(g)))
-        def _():
-            whole_copy(done.at[g], back_out.at[g], back_in.at[g]).wait_recv()
-            whole_copy(grads.at[g], red_out.at[g], red_in.at[g]).wait_send()
-
-        for i in range(per_group):
-            sums_ref[g * per_group + i] = done[g, i]
-            sums_ref[heads + g * per_group + i] = done[g, per_group + i]
-
-    put_out = pltpu.make_async_copy(qin, out_ref, out_sem)
+    def reduce_start(r):
+        for o in range(owners):
+
+            @pl.when(middle + o * stride != flat)
+            def _(o=o):
+                to_owner(r, o).start()
+
+    def reduce_own(r):
+        @pl.when(inside)
+        def _():
+            slots_now = arriving(r)
+            whole_copy(slots_now, red_out.at[r], red_in.at[r]).wait_recv()
+            done[share(r, part)] = grads[share(r, part)] + jnp.sum(slots_now[...], 0)
+            each_other(axes, lambda where: to_all(r, where).start())
+
+    def reduce_end(r):
+        first, size = rounds[r]
+        per = size // owners
+        every, others = pl.ds(first, size), pl.ds(first, size - per)
+
+        @pl.when(inside)
+        def _():
+            if owners > 1:
+                whole_copy(done.at[others], back_out.at[r], back_in.at[r]).wait_recv()
+                whole_copy(grads.at[others], red_out.at[r], red_in.at[r]).wait_send()
+            whole_copy(arriving(r), back_out.at[r], back_in.at[r]).wait_send()
+
+        @pl.when(jnp.logical_not(inside))
+        def _():
+            whole_copy(done.at[every], back_out.at[r], back_in.at[r]).wait_recv()
+            whole_copy(grads.at[every], red_out.at[r], red_in.at[r]).wait_send()
+
+        sums_ref[every] = done[every]
 
     def write_out(n):
-        qin[at(n)] = by_head(oh[:, at(n)])
+        out_ref[at(n)] = by_head(oh[:, at(n)])
 
     with jax.named_scope("write_out"):
         for n in range(1, tiles):
@@ -618,32 +639,32 @@
             halo_wait(g, 0)
         with jax.named_scope("first_keys"):
             kx[first:last, at(0)] = by_head(halo[g, 0])
-            over_heads(first, last, UNROLL, first_keys)
+            over_heads(first, last, LATE, first_keys)
         with jax.named_scope("halo_v"):
             halo_wait(g, 1)
         with jax.named_scope("first_values"):
             vx[first:last, at(0)] = by_head(halo[g, 1])
-            over_heads(first, last, UNROLL, first_values)
+            over_heads(first, last, LATE, first_values)
         with jax.named_scope("send_ds"):
             message_start(g)
         with jax.named_scope("local_keys"):
             over_heads(first, last, UNROLL, local_keys)
     with jax.named_scope("write_0"):
         write_out(0)
-        put_out.start()
+    reduce_start(0)
     for g in range(GROUPS):
         with jax.named_scope("wait_ds"):
             message_sum(g)
         with jax.named_scope("final_keys"):
-            over_heads(g * per_group, (g + 1) * per_group, UNROLL, final_keys)
+            over_heads(g * per_group, (g + 1) * per_group, LATE, final_keys)
         with jax.named_scope("red_start"):
-            reduce_start(g)
+            reduce_start(1 + g)
     with jax.named_scope("red_own"):
-        for g in range(GROUPS):
-            reduce_own(g)
+        for r in range(1 + GROUPS):
+            reduce_own(r)
     with jax.named_scope("red_end"):
-        for g in range(GROUPS):
-            reduce_end(g)
+        for r in range(1 + GROUPS):
+            reduce_end(r)
     with jax.named_scope("sent"):
         @pl.when(me < peers - 1)
         def _():
@@ -652,29 +673,21 @@
         states_sent()
         for g in range(GROUPS):
             message_sent(g)
-        put_out.wait()
-
-
-def finish_kernel(rows_hbm, sums_hbm, out_hbm, gq_hbm, gk_hbm, rows, sums, in_sem, out_sem):
-    tokens = rows.shape[0]
+
+
+def finish_kernel(rows_ref, sums_ref, out_hbm, gq_hbm, gk_hbm, sem):
     heads = gq_hbm.shape[0]
-    parts = [pl.ds(i * heads, heads) for i in range(2)]
-    sums_in = pltpu.make_async_copy(sums_hbm, sums, in_sem.at[PIECES])
-    chunks = [pl.ds(i * (tokens // PIECES), tokens // PIECES) for i in range(PIECES)]
-    rows_in = [pltpu.make_async_copy(rows_hbm.at[c], rows.at[c], in_sem.at[i]) for i, c in enumerate(chunks)]
-    rows_out = [pltpu.make_async_copy(rows.at[c], out_hbm.at[c], out_sem.at[i]) for i, c in enumerate(chunks)]
-    outs = [(sums.at[parts[0]], gq_hbm), (sums.at[parts[1]], gk_hbm)]
-    sums_out = [pltpu.make_async_copy(a, b, out_sem.at[PIECES + i]) for i, (a, b) in enumerate(outs)]
-    sums_in.start()
-    for copy in rows_in:
+    tokens = rows_ref.shape[0] // PARTS
+    copies = [
+        pltpu.make_async_copy(sums_ref.at[pl.ds(0, heads)], gq_hbm, sem.at[PARTS]),
+        pltpu.make_async_copy(sums_ref.at[pl.ds(heads, heads)], gk_hbm, sem.at[PARTS + 1]),
+    ]
+    for i in range(PARTS):
+        some = pl.ds(i * tokens, tokens)
+        copies.append(pltpu.make_async_copy(rows_ref.at[some], out_hbm.at[some], sem.at[i]))
+    for copy in copies:
         copy.start()
-    sums_in.wait()
-    for copy in sums_out:
-        copy.start()
-    for i in range(PIECES):
-        rows_in[i].wait()
-        rows_out[i].start()
-    for copy in sums_out + rows_out:
+    for copy in copies:
         copy.wait()
 
 
@@ -687,8 +700,7 @@
     peers = lax.axis_size("seq")
     count = peers * lax.axis_size("batch")
     per_group = heads // GROUPS
-    chunks = 2 * per_group
-    owners, per = owners_of(count, chunks)
+    owners, _, _ = owners_of(count, per_group)
     block = (per_group + 2, rank, width)
     hbm = pl.BlockSpec(memory_space=pltpu.HBM)
     vmem = pl.BlockSpec(memory_space=pltpu.VMEM)
@@ -697,12 +709,12 @@
     tiled = pltpu.VMEM((tiles + 1, heads, rank, width), F32)
     states = (heads + 2, rank, width)
     packed = pltpu.VMEM((heads, rank, width), BF16)
-    operands = [q_rows, k_rows, v_rows, cot, jnp.swapaxes(query_map, 1, 2), jnp.swapaxes(key_map, 1, 2)]
+    operands = [keep_count[0], q_rows, k_rows, v_rows, cot, jnp.swapaxes(query_map, 1, 2), jnp.swapaxes(key_map, 1, 2)]
     rows, sums = pl.pallas_call(
         functools.partial(layer_kernel, "seq", axes),
         name="layer",
         in_specs=[hbm] * 7,
-        out_specs=[hbm, vmem],
+        out_specs=[vmem, vmem],
         out_shape=[
             jax.ShapeDtypeStruct((tokens, heads, width), BF16),
             jax.ShapeDtypeStruct((2 * heads, rank, width), F32),
@@ -724,38 +736,36 @@
             packed, packed,
             pltpu.VMEM((heads, 2 * TILE, TILE), BF16),
             small,
+            pltpu.VMEM((GROUPS, 2, TILE, per_group, width), BF16),
             pltpu.VMEM(states, F32),
             pltpu.VMEM((3,) + states, BF16),
             pltpu.VMEM((2,) + states, BF16),
             pltpu.VMEM((peers // 2,) + states, BF16),
             pltpu.VMEM((GROUPS,) + block, BF16),
             pltpu.VMEM((GROUPS, peers) + block, BF16),
-            pltpu.VMEM((GROUPS, chunks, rank, width), F32),
-            pltpu.VMEM((GROUPS, count - 1, per, rank, width), F32),
-            pltpu.VMEM((GROUPS, chunks, rank, width), F32),
-            dma((4,)), dma((3,)), dma(()), dma((GROUPS, 2)), dma((2,)), dma((2,)),
+            pltpu.VMEM((2 * heads, rank, width), F32),
+            pltpu.VMEM((count - 1, heads // owners, rank, width), F32),
+            pltpu.VMEM((GROUPS, count - 1, per_group // owners, rank, width), F32),
+            pltpu.VMEM((2 * heads, rank, width), F32),
+            dma((4,)), dma((GROUPS, 2)), dma((3,)), dma(()), dma((GROUPS, 2)), dma((2,)), dma((2,)),
             dma((peers // 2,)), dma((peers // 2,)), dma((GROUPS, peers)), dma((GROUPS, peers)),
-            dma((GROUPS,)), dma((GROUPS,)), dma((GROUPS,)), dma((GROUPS,)), dma(()),
+            dma((1 + GROUPS,)), dma((1 + GROUPS,)), dma((1 + GROUPS,)), dma((1 + GROUPS,)),
         ],
         compiler_params=pltpu.CompilerParams(
             collective_id=0, has_side_effects=True, vmem_limit_bytes=VMEM_LIMIT
         ),
-    )(keep_count[0], *operands)
+    )(*[pltpu.with_memory_space_constraint(x, pltpu.HBM) for x in operands])
     out, gq, gk = pl.pallas_call(
         finish_kernel,
         name="finish",
-        in_specs=[hbm, hbm],
+        in_specs=[vmem, vmem],
         out_specs=[hbm, hbm, hbm],
         out_shape=[
             jax.ShapeDtypeStruct((tokens, heads, width), BF16),
             jax.ShapeDtypeStruct((heads, rank, width), F32),
             jax.ShapeDtypeStruct((heads, rank, width), F32),
         ],
-        scratch_shapes=[
-            pltpu.VMEM((tokens, heads, width), BF16),
-            pltpu.VMEM((2 * heads, rank, width), F32),
-            dma((PIECES + 1,)), dma((PIECES + 2,)),
-        ],
+        scratch_shapes=[dma((PARTS + 2,))],
         compiler_params=pltpu.CompilerParams(vmem_limit_bytes=VMEM_LIMIT),
     )(rows, sums)
     return out[None], jnp.swapaxes(gq, 1, 2), jnp.swapaxes(gk, 1, 2)

time: 54.2 us -> 49.8 us (0.919)
  Pallas kernels: 53.4 us -> 49 us
    pallas_call x1, Pallas kernels: 50.9 us -> 47.6 us  [body(): pl.pallas_call(functools.partial(layer_kernel, 'seq', axes), name='layer'...]
    pallas_call x1, Pallas kernels: 2.52 us -> 1.41 us  [body(): pl.pallas_call(finish_kernel, name='finish', in_specs=[vmem, vmem], out_s...]
where the time goes in v3:
time: 49.8 us; the launch traced here: 49.6 us
  Pallas kernels  49 us (98%)
  between operations  0.64 us (1%)
    pallas_call x1, Pallas kernels, body(): pl.pallas_call(functools.partial(layer_kernel, 'seq', axes), name='layer'...  47.6 us
    pallas_call x1, Pallas kernels, body(): pl.pallas_call(finish_kernel, name='finish', in_specs=[vmem, vmem], out_s...  1.41 us

profile of v3, /device:TPU:0, one launch (start us, length us, event | category | flops | bytes accessed | tf_op | source)
XLA Modules:
  0.0 49.6 jit_solution(5372521237316818800)
XLA Ops:
  0.6 47.6 %layer.1 = (bf16[512,16,128]{2,1,0:T(8,128)(2,1)S(1)}, f32[32,8,128]{2,1,0:T(8,128)S(1)}) custom-call(s32[16,32]{1,0:T(8,128)} %bitcast.16, bf16[512,16,128]{2,1,0:T(8,128)(2,1)} %bitcast.10, bf16[512,16,128]{2,1,0:T(8,128)(2,1)} %bitcast.11, bf16[512,16,128]{2,1,0:T(8,128)(2,1)} %bitcast.12, bf16[512,16,128]{2,1,0:T(8,128)(2,1)} %bitcast.13, ...), custom_call_target="tpu_custom_call" | custom-call | tf_op jit(solution)/shard_map/layer/pallas_call | solution.py:713
  48.2 1.4 %finish.1 = (bf16[512,16,128]{2,1,0:T(8,128)(2,1)}, f32[16,8,128]{2,1,0:T(8,128)}, f32[16,8,128]{2,1,0:T(8,128)}) custom-call(bf16[512,16,128]{2,1,0:T(8,128)(2,1)S(1)} %get-tuple-element.8.rows_ref, f32[32,8,128]{2,1,0:T(8,128)S(1)} %get-tuple-element.9.sums_ref), custom_call_target="tpu_custom_call" | custom-call | tf_op jit(solution)/shard_map/finish/pallas_call | solution.py:758

commit v4 on v3

--- a/solution.py
+++ b/solution.py
@@ -14,12 +14,10 @@
 MASKED = -1e30
 F32 = jnp.float32
 BF16 = jnp.bfloat16
-GROUPS = 2
 UNROLL = 4
 CUTS = 4
 EARLY_EVEN = 9
 EARLY_ODD = 3
-LATE = 8
 PARTS = 4
 VMEM_LIMIT = 50 * 1024 * 1024
 
@@ -109,6 +107,11 @@
     return pl.ds(tile * TILE, count * TILE)
 
 
+def groups_of(heads):
+    half, quarter = heads // 2, heads // 4
+    return [(0, half), (half, quarter), (half + quarter, quarter)]
+
+
 def owners_of(count, chunks):
     owners = min(count, chunks)
     stride = 2 if count >= 2 * owners else 1
@@ -119,14 +122,15 @@
     seq, axes, counts_hbm, q_hbm, k_hbm, v_hbm, c_hbm, wq_hbm, wk_hbm, out_ref, sums_ref,
     qin, kin, vin, cin, kx, vx, vt, qx, ct, oh, halo, num, rows, preq, sigk, sall, nall, skept, nkept,
     sin, nin, dsb, dnb, gaf, naf, counts_ref, wq_ref, wk_ref, prob, fkept, sent_halo,
-    own, state_out, state_in, even_in, mine, slots, grads, qslots, kslots, done,
+    own, state_out, state_in, even_in, mine, slots, grads, early_slots, late_slots, done,
     in_sem, edge_sem, small_sem, halo_out, halo_in, pair_out, pair_in, even_out_sem, even_in_sem,
     msg_out, msg_in, red_out, red_in, back_out, back_in,
 ):
     tokens, heads, width = q_hbm.shape
     rank = wq_hbm.shape[1]
     tiles = tokens // TILE
-    per_group = heads // GROUPS
+    groups = groups_of(heads)
+    half = groups[0][1]
     factor = LOG2E / math.sqrt(width)
     me = lax.axis_index(seq)
     peers = lax.axis_size(seq)
@@ -140,9 +144,8 @@
 
     early = [
         pltpu.make_async_copy(
-            hbm.at[pl.ds(tokens - TILE, TILE), pl.ds(g * per_group, per_group)], sent_halo.at[g, i], edge_sem.at[g, i]
+            hbm.at[pl.ds(tokens - TILE, TILE), pl.ds(0, half)], sent_halo.at[i], edge_sem.at[i]
         )
-        for g in range(GROUPS)
         for i, hbm in enumerate((k_hbm, v_hbm))
     ]
     for copy in early:
@@ -163,17 +166,27 @@
     @pl.when(me == 0)
     def _():
         halo[...] = jnp.zeros_like(halo)
+        blank = jnp.zeros((heads - half, TILE, width), BF16)
+        kx[half:, at(0)] = blank
+        vx[half:, at(0)] = blank
         state_in[0] = jnp.zeros_like(state_in[0])
 
     even = lax.rem(me, 2) == 0
     cut = TILE // CUTS
-    pieces = [(g, i, r) for g in range(GROUPS) for i in range(2) for r in range(CUTS)]
+    pieces = [(0, i, r) for i in range(2) for r in range(CUTS)]
+    for g, (first, size) in enumerate(groups[1:], 1):
+        pieces += [(g, i, h) for i in range(2) for h in range(first, first + size, 2)]
 
     def halo_copy(g, i, r):
+        if g:
+            both = (kx, vx)[i].at[pl.ds(r, 2)]
+            src, dst = both.at[:, at(tiles)], both.at[:, at(0)]
+        else:
+            src, dst = sent_halo.at[i, pl.ds(r * cut, cut)], halo.at[i, pl.ds(r * cut, cut)]
         return pltpu.make_async_remote_copy(
-            src_ref=sent_halo.at[g, i, pl.ds(r * cut, cut)],
-            dst_ref=halo.at[g, i, pl.ds(r * cut, cut)],
-            send_sem=halo_out,
+            src_ref=src,
+            dst_ref=dst,
+            send_sem=halo_out.at[1 + i if g else 0],
             recv_sem=halo_in.at[g, i],
             device_id=place(lax.rem(me + 1, peers), sq),
             device_id_type=pl.DeviceIdType.MESH,
@@ -192,9 +205,10 @@
     def halo_wait(g, i):
         @pl.when(me > 0)
         def _():
-            whole_copy(halo.at[g, i], halo_out, halo_in.at[g, i]).wait_recv()
-
-    for copy in early[:2]:
+            landed = (kx, vx)[i].at[pl.ds(*groups[g]), at(0)] if g else halo.at[i]
+            whole_copy(landed, halo_out.at[0], halo_in.at[g, i]).wait_recv()
+
+    for copy in early:
         copy.wait()
     with jax.named_scope("barrier"):
         pl.semaphore_wait(barrier, count - 1)
@@ -209,9 +223,6 @@
     first_group = 2 * CUTS
     halo_start(even, pieces[:first_group])
     halo_start(odd, pieces[:EARLY_ODD])
-    for copy in early[2:]:
-        copy.wait()
-    halo_start(even, pieces[first_group:EARLY_EVEN])
 
     def count_before(h, e):
         if e:
@@ -315,23 +326,28 @@
             pair_copy(0, me + 1).wait_send()
 
     def message(g, sender, target):
+        blocks = pl.ds(0, groups[g][1] + 1)
         return pltpu.make_async_remote_copy(
-            src_ref=mine.at[g],
-            dst_ref=slots.at[g, sender],
+            src_ref=mine.at[g, blocks],
+            dst_ref=slots.at[g, sender, blocks],
             send_sem=msg_out.at[g, target],
             recv_sem=msg_in.at[g, sender],
             device_id=place(target, sq),
             device_id_type=pl.DeviceIdType.MESH,
         )
 
+    def twice(i):
+        return (lane == i) | (lane == width // 2 + i)
+
     def message_start(g):
+        first, size = groups[g]
         every = range(1, tiles + 1)
         packed = jnp.zeros((rank, width), F32)
-        for i in range(per_group):
-            h = g * per_group + i
-            mine[g, i] = sum(dsb[j, h] for j in every).astype(BF16)
-            packed = jnp.where(lane == i, sum(dnb[j, h] for j in every), packed)
-        mine[g, per_group], mine[g, per_group + 1] = halves(packed)
+        for i in range(size):
+            mine[g, i] = sum(dsb[j, first + i] for j in every).astype(BF16)
+            packed = jnp.where(twice(i), sum(dnb[j, first + i] for j in every), packed)
+        top = packed.astype(BF16).astype(F32)
+        mine[g, size] = jnp.where(lane < width // 2, top, packed - top).astype(BF16)
 
         def send(p, carry):
             message(g, me, p).start()
@@ -347,15 +363,16 @@
         lax.fori_loop(0, me, sent, 0)
 
     def message_sum(g):
+        first, size = groups[g]
+
         def received(p, total):
             message(g, p, lax.rem(me + 1, peers)).wait_recv()
-            return total + slots[g, p].astype(F32)
-
-        total = lax.fori_loop(me + 1, peers, received, jnp.zeros((per_group + 2, rank, width), F32))
-        norms = total[per_group] + total[per_group + 1]
-        for i in range(per_group):
-            gaf[g * per_group + i] = total[i]
-            naf[g * per_group + i] = spread(jnp.where(lane == i, norms, 0.0))
+            return total + slots[g, p, : size + 1].astype(F32)
+
+        total = lax.fori_loop(me + 1, peers, received, jnp.zeros((size + 1, rank, width), F32))
+        for i in range(size):
+            gaf[first + i] = total[i]
+            naf[first + i] = spread(jnp.where(twice(i), total[size], 0.0))
 
     def spread(x):
         return jnp.broadcast_to(jnp.sum(x, 1, keepdims=True), (rank, width))
@@ -372,6 +389,7 @@
         loads[0].wait()
         for n in range(tiles):
             kx[:, at(n + 1)] = by_head(kin[at(n)])
+    halo_start(even, pieces[first_group:EARLY_EVEN])
     with jax.named_scope("values"):
         loads[1].wait()
         for n in range(tiles):
@@ -540,8 +558,9 @@
         for i, h in enumerate(hs):
             grads[heads + h] += gk[i]
 
-    owners, stride, middle = owners_of(count, per_group)
-    rounds = [(0, heads)] + [(heads + g * per_group, per_group) for g in range(GROUPS)]
+    owners, stride, middle = owners_of(count, groups[-1][1])
+    rounds = groups + [(heads + first, size) for first, size in groups]
+    key_round = len(groups)
     ahead = flat - middle + count * stride
     part = lax.rem(ahead // stride, owners)
     inside = (flat >= middle) & (flat < middle + owners * stride) & (lax.rem(ahead, stride) == 0)
@@ -552,7 +571,8 @@
         return pl.ds(first + o * per, per)
 
     def arriving(r):
-        return kslots.at[r - 1] if r else qslots
+        kind, g = divmod(r, key_round)
+        return late_slots.at[kind, g - 1] if g else early_slots.at[kind]
 
     def to_owner(r, o):
         target = middle + o * stride
@@ -633,45 +653,50 @@
         weighted(hs, 1, [prob[h] for h in hs])
         combine(hs, 1)
 
-    for g in range(GROUPS):
-        first, last = g * per_group, (g + 1) * per_group
+    for g, (first, size) in enumerate(groups):
+        last = first + size
         with jax.named_scope("halo_k"):
             halo_wait(g, 0)
         with jax.named_scope("first_keys"):
-            kx[first:last, at(0)] = by_head(halo[g, 0])
-            over_heads(first, last, LATE, first_keys)
+            if g == 0:
+                kx[:half, at(0)] = by_head(halo[0])
+            over_heads(first, last, size, first_keys)
         with jax.named_scope("halo_v"):
             halo_wait(g, 1)
         with jax.named_scope("first_values"):
-            vx[first:last, at(0)] = by_head(halo[g, 1])
-            over_heads(first, last, LATE, first_values)
+            if g == 0:
+                vx[:half, at(0)] = by_head(halo[1])
+            over_heads(first, last, size, first_values)
         with jax.named_scope("send_ds"):
             message_start(g)
+            reduce_start(g)
         with jax.named_scope("local_keys"):
             over_heads(first, last, UNROLL, local_keys)
     with jax.named_scope("write_0"):
         write_out(0)
-    reduce_start(0)
-    for g in range(GROUPS):
+    for g, (first, size) in enumerate(groups):
         with jax.named_scope("wait_ds"):
             message_sum(g)
         with jax.named_scope("final_keys"):
-            over_heads(g * per_group, (g + 1) * per_group, LATE, final_keys)
+            over_heads(first, first + size, size, final_keys)
         with jax.named_scope("red_start"):
-            reduce_start(1 + g)
+            reduce_start(key_round + g)
     with jax.named_scope("red_own"):
-        for r in range(1 + GROUPS):
+        for r in range(len(rounds)):
             reduce_own(r)
     with jax.named_scope("red_end"):
-        for r in range(1 + GROUPS):
+        for r in range(len(rounds)):
             reduce_end(r)
     with jax.named_scope("sent"):
         @pl.when(me < peers - 1)
         def _():
-            whole_copy(halo, halo_out, halo_in.at[0, 0]).wait_send()
+            whole_copy(halo, halo_out.at[0], halo_in.at[0, 0]).wait_send()
+            for i, ref in enumerate((kx, vx)):
+                rest = ref.at[pl.ds(half, heads - half), at(tiles)]
+                whole_copy(rest, halo_out.at[1 + i], halo_in.at[0, 0]).wait_send()
 
         states_sent()
-        for g in range(GROUPS):
+        for g in range(len(groups)):
             message_sent(g)
 
 
@@ -699,9 +724,8 @@
     axes = ("seq", "batch")
     peers = lax.axis_size("seq")
     count = peers * lax.axis_size("batch")
-    per_group = heads // GROUPS
-    owners, _, _ = owners_of(count, per_group)
-    block = (per_group + 2, rank, width)
+    half, quarter = groups_of(heads)[0][1], groups_of(heads)[-1][1]
+    owners, _, _ = owners_of(count, quarter)
     hbm = pl.BlockSpec(memory_space=pltpu.HBM)
     vmem = pl.BlockSpec(memory_space=pltpu.VMEM)
     dma = pltpu.SemaphoreType.DMA
@@ -726,7 +750,7 @@
             pltpu.VMEM((heads, tokens, width), BF16),
             pltpu.VMEM((heads, width, tokens), BF16),
             pltpu.VMEM((heads, tokens, width), BF16),
-            pltpu.VMEM((GROUPS, 2, TILE, per_group, width), BF16),
+            pltpu.VMEM((2, TILE, half, width), BF16),
             pltpu.VMEM((heads, width, tokens), F32),
             pltpu.VMEM((heads, 8, tokens), F32),
             pltpu.VMEM((heads, rank, tokens), F32),
@@ -736,20 +760,20 @@
             packed, packed,
             pltpu.VMEM((heads, 2 * TILE, TILE), BF16),
             small,
-            pltpu.VMEM((GROUPS, 2, TILE, per_group, width), BF16),
+            pltpu.VMEM((2, TILE, half, width), BF16),
             pltpu.VMEM(states, F32),
             pltpu.VMEM((3,) + states, BF16),
             pltpu.VMEM((2,) + states, BF16),
             pltpu.VMEM((peers // 2,) + states, BF16),
-            pltpu.VMEM((GROUPS,) + block, BF16),
-            pltpu.VMEM((GROUPS, peers) + block, BF16),
+            pltpu.VMEM((3, half + 1, rank, width), BF16),
+            pltpu.VMEM((3, peers, half + 1, rank, width), BF16),
             pltpu.VMEM((2 * heads, rank, width), F32),
-            pltpu.VMEM((count - 1, heads // owners, rank, width), F32),
-            pltpu.VMEM((GROUPS, count - 1, per_group // owners, rank, width), F32),
+            pltpu.VMEM((2, count - 1, half // owners, rank, width), F32),
+            pltpu.VMEM((2, 2, count - 1, quarter // owners, rank, width), F32),
             pltpu.VMEM((2 * heads, rank, width), F32),
-            dma((4,)), dma((GROUPS, 2)), dma((3,)), dma(()), dma((GROUPS, 2)), dma((2,)), dma((2,)),
-            dma((peers // 2,)), dma((peers // 2,)), dma((GROUPS, peers)), dma((GROUPS, peers)),
-            dma((1 + GROUPS,)), dma((1 + GROUPS,)), dma((1 + GROUPS,)), dma((1 + GROUPS,)),
+            dma((4,)), dma((2,)), dma((3,)), dma((3,)), dma((3, 2)), dma((2,)), dma((2,)),
+            dma((peers // 2,)), dma((peers // 2,)), dma((3, peers)), dma((3, peers)),
+            dma((6,)), dma((6,)), dma((6,)), dma((6,)),
         ],
         compiler_params=pltpu.CompilerParams(
             collective_id=0, has_side_effects=True, vmem_limit_bytes=VMEM_LIMIT

time: 49.8 us -> 49.4 us (level)
  no operation moved by 1% of the time
where the time goes in v4:
time: 49.4 us; the launch traced here: 49.2 us
  Pallas kernels  48.6 us (98%)
  between operations  0.64 us (1%)
    pallas_call x1, Pallas kernels, body(): pl.pallas_call(functools.partial(layer_kernel, 'seq', axes), name='layer'...  47.2 us
    pallas_call x1, Pallas kernels, body(): pl.pallas_call(finish_kernel, name='finish', in_specs=[vmem, vmem], out_s...  1.41 us

profile of v4, /device:TPU:0, one launch (start us, length us, event | category | flops | bytes accessed | tf_op | source)
XLA Modules:
  0.0 49.2 jit_solution(4896755523723172429)
XLA Ops:
  0.6 47.2 %layer.1 = (bf16[512,16,128]{2,1,0:T(8,128)(2,1)S(1)}, f32[32,8,128]{2,1,0:T(8,128)S(1)}) custom-call(s32[16,32]{1,0:T(8,128)} %bitcast.16, bf16[512,16,128]{2,1,0:T(8,128)(2,1)} %bitcast.10, bf16[512,16,128]{2,1,0:T(8,128)(2,1)} %bitcast.11, bf16[512,16,128]{2,1,0:T(8,128)(2,1)} %bitcast.12, bf16[512,16,128]{2,1,0:T(8,128)(2,1)} %bitcast.13, ...), custom_call_target="tpu_custom_call" | custom-call | tf_op jit(solution)/shard_map/layer/pallas_call | solution.py:737
  47.8 1.4 %finish.1 = (bf16[512,16,128]{2,1,0:T(8,128)(2,1)}, f32[16,8,128]{2,1,0:T(8,128)}, f32[16,8,128]{2,1,0:T(8,128)}) custom-call(bf16[512,16,128]{2,1,0:T(8,128)(2,1)S(1)} %get-tuple-element.8.rows_ref, f32[32,8,128]{2,1,0:T(8,128)S(1)} %get-tuple-element.9.sums_ref), custom_call_target="tpu_custom_call" | custom-call | tf_op jit(solution)/shard_map/finish/pallas_call | solution.py:782

commit v5 on v4

--- a/solution.py
+++ b/solution.py
@@ -14,7 +14,7 @@
 MASKED = -1e30
 F32 = jnp.float32
 BF16 = jnp.bfloat16
-UNROLL = 4
+UNROLL = 8
 CUTS = 4
 EARLY_EVEN = 9
 EARLY_ODD = 3
@@ -378,6 +378,8 @@
         return jnp.broadcast_to(jnp.sum(x, 1, keepdims=True), (rank, width))
 
     def over_heads(first, last, step, act):
+        step = min(step, last - first)
+
         def block(i, carry):
             act([first + i * step + u for u in range(step)])
             return carry

time: 49.4 us -> 50.8 us (1.028)
  Pallas kernels: 48.6 us -> 50 us
    pallas_call x1, Pallas kernels: 47.2 us -> 48.6 us  [body(): pl.pallas_call(functools.partial(layer_kernel, 'seq', axes), name='layer'...]
where the time goes in v5:
time: 50.8 us; the launch traced here: 50.6 us
  Pallas kernels  50 us (98%)
  between operations  0.64 us (1%)
    pallas_call x1, Pallas kernels, body(): pl.pallas_call(functools.partial(layer_kernel, 'seq', axes), name='layer'...  48.6 us
    pallas_call x1, Pallas kernels, body(): pl.pallas_call(finish_kernel, name='finish', in_specs=[vmem, vmem], out_s...  1.41 us

profile of v5, /device:TPU:0, one launch (start us, length us, event | category | flops | bytes accessed | tf_op | source)
XLA Modules:
  0.0 50.6 jit_solution(2348751905339743639)
XLA Ops:
  0.6 48.6 %layer.1 = (bf16[512,16,128]{2,1,0:T(8,128)(2,1)S(1)}, f32[32,8,128]{2,1,0:T(8,128)S(1)}) custom-call(s32[16,32]{1,0:T(8,128)} %bitcast.16, bf16[512,16,128]{2,1,0:T(8,128)(2,1)} %bitcast.10, bf16[512,16,128]{2,1,0:T(8,128)(2,1)} %bitcast.11, bf16[512,16,128]{2,1,0:T(8,128)(2,1)} %bitcast.12, bf16[512,16,128]{2,1,0:T(8,128)(2,1)} %bitcast.13, ...), custom_call_target="tpu_custom_call" | custom-call | tf_op jit(solution)/shard_map/layer/pallas_call | solution.py:739
  49.2 1.4 %finish.1 = (bf16[512,16,128]{2,1,0:T(8,128)(2,1)}, f32[16,8,128]{2,1,0:T(8,128)}, f32[16,8,128]{2,1,0:T(8,128)}) custom-call(bf16[512,16,128]{2,1,0:T(8,128)(2,1)S(1)} %get-tuple-element.8.rows_ref, f32[32,8,128]{2,1,0:T(8,128)S(1)} %get-tuple-element.9.sums_ref), custom_call_target="tpu_custom_call" | custom-call | tf_op jit(solution)/shard_map/finish/pallas_call | solution.py:784
